TPU v7x, 32 devices: a whole 2x2x4 slice. The times are simulated.
32 devices in a mesh: enc: 8 (over z, x), section: 2 (over core), llmdp: 2 (over y).
Axes of the slice: x: 2, y: 2, z: 4, core: 2. Of those that a mesh axis runs over, the one named last changes fastest.
Arguments:
- patches: bfloat16 [2048, 3200], P('enc', ('section', 'llmdp')), may hold values from -6 to 6
- gain: float32 [3200], replicated, may hold values from 0.25 to 1.75
- shift: float32 [3200], replicated, may hold values from -3 to 3
- proj_weight: bfloat16 [3200, 8192], P('enc', ('section', 'llmdp')), may hold values from -0.109375 to 0.109375
- llm_rank: int32 [2048, 1], P('enc'), may hold values from 0 to 7; in each aligned block of 256 rows (0 to 255, 256 to 511, ...) at most 96 rows name the same one
- embed_grad: bfloat16 [6144, 8192], P('enc', ('section', 'llmdp')), may hold values from -0.59765625 to 0.59765625
Outputs:
- embeds_recv: bfloat16 [6144, 8192], P('enc', ('section', 'llmdp'))
- hidden_state_gradient: bfloat16 [2048, 3200], P('enc', ('section', 'llmdp'))
- grad_weight: float32 [3200, 8192], P('enc', ('section', 'llmdp'))
- gain_gradient: float32 [3200], P(('section', 'llmdp'))
- grad_shift: float32 [3200], P(('section', 'llmdp'))
Inputs may be any that keep to these rules, and one draw needn't show every extreme that they name: `llm_rank`: among the 256 rows of one device, at most 96 name the same owner, a bound that some block reaches.
All inputs are finite; a program needn't handle non-finite values.
Results may differ from a plain program's by a relative error of at most 0.018.
Values may be sent and summed in bfloat16 or wider, within the bound.
A program may use at most 128 MiB of HBM per device.

v0:
```python
import jax
import jax.numpy as jnp
from jax import lax
from jax.sharding import PartitionSpec as P

EPSILON = 1e-05


MAX_BLOCK = 2


def block_size(senders, out_cols):
    size = MAX_BLOCK
    while size > 1 and (senders % size or senders == size or out_cols % (size * 128)):
        size //= 2
    return size


def body(patches, gain, shift, proj_weight, llm_rank, embed_grad):
    features = ("section", "llmdp")
    own_rows, owned_width = patches.shape
    width = gain.shape[0]
    weight_rows, out_cols = proj_weight.shape
    senders = lax.axis_size("enc")
    block = block_size(senders, out_cols)
    near = [[b * block + i for i in range(block)] for b in range(senders // block)]
    far = [[b * block + i for b in range(senders // block)] for i in range(block)]

    def near_exchange(x, split, concat):
        return lax.all_to_all(x, "enc", split, concat, axis_index_groups=near, tiled=True)

    column_start = lax.axis_index(features) * owned_width
    gain_own = lax.dynamic_slice_in_dim(gain, column_start, owned_width, 0)

    weight_part = near_exchange(proj_weight, 1, 0)
    weight = lax.all_gather(weight_part, "enc", axis=0, axis_index_groups=far, tiled=True)

    block_rows = lax.all_gather(patches, "enc", axis=0, axis_index_groups=near, tiled=True)
    complete_rows = lax.all_gather(block_rows, features, axis=1, tiled=True).astype(jnp.float32)
    row_average = jnp.mean(complete_rows, 1, keepdims=True)
    variance = jnp.mean(complete_rows * complete_rows, 1, keepdims=True) - row_average * row_average
    inverse_deviation = lax.rsqrt(variance + EPSILON)
    standardized = (complete_rows - row_average) * inverse_deviation
    normed = (standardized * gain + shift).astype(jnp.bfloat16)

    row_start = (lax.axis_index("enc") % block) * own_rows
    average_own = lax.dynamic_slice_in_dim(row_average, row_start, own_rows, 0)
    deviation_own = lax.dynamic_slice_in_dim(inverse_deviation, row_start, own_rows, 0)
    standardized_owned = (patches.astype(jnp.float32) - average_own) * deviation_own

    most_slots = embed_grad.shape[0] // senders
    target = llm_rank[:, 0]
    owners = jnp.arange(senders, dtype=jnp.int32)
    hits = (target[:, None] == owners[None, :]).astype(jnp.int32)
    rank = jnp.sum((jnp.cumsum(hits, 0) - hits) * hits, 1)
    slot = target * most_slots + rank

    def enc_exchange(x):
        return lax.all_to_all(
            x.reshape(senders, most_slots, out_cols), "enc", split_axis=0, concat_axis=0, tiled=True
        ).reshape(senders * most_slots, out_cols)

    d_embed = near_exchange(enc_exchange(embed_grad)[slot], 1, 0)
    grad_part = lax.psum_scatter(
        lax.dot_general(
            normed, d_embed, (((0,), (0,)), ((), ())), preferred_element_type=jnp.float32
        ).astype(jnp.bfloat16),
        "enc",
        scatter_dimension=0,
        axis_index_groups=far,
        tiled=True,
    )
    grad_weight = near_exchange(grad_part, 0, 1).astype(jnp.float32)

    embed_part = jnp.dot(normed, weight, preferred_element_type=jnp.float32).astype(jnp.bfloat16)
    embed = near_exchange(embed_part, 0, 1)
    outgoing = jnp.zeros((senders * most_slots, out_cols), jnp.bfloat16).at[slot].set(embed)
    embeds_recv = enc_exchange(outgoing)

    partial_grad = lax.dot_general(
        d_embed, weight, (((1,), (1,)), ((), ())), preferred_element_type=jnp.float32
    )
    group_count = width // owned_width
    pieces = partial_grad.astype(jnp.bfloat16).reshape(block * own_rows, group_count, owned_width)
    columns = lax.all_to_all(pieces, features, split_axis=1, concat_axis=1, tiled=True)
    column_sum = jnp.sum(columns.astype(jnp.float32), 1).astype(jnp.bfloat16)
    shares = near_exchange(column_sum.reshape(block, own_rows, owned_width), 0, 0)
    owned_normalized_gradient = jnp.sum(shares.astype(jnp.float32), 0)
    owned_centered_gradient = owned_normalized_gradient * gain_own
    mean_sum, cross_sum = lax.psum(
        (
            jnp.sum(owned_centered_gradient, 1),
            jnp.sum(owned_centered_gradient * standardized_owned, 1),
        ),
        features,
    )
    gradient_row_average = (mean_sum / width)[:, None]
    gradient_cross_product = (cross_sum / width)[:, None]
    hidden_state_gradient = (
        deviation_own
        * (
            owned_centered_gradient
            - gradient_row_average
            - standardized_owned * gradient_cross_product
        )
    ).astype(jnp.bfloat16)
    gain_gradient, grad_shift = lax.psum(
        (
            jnp.sum(owned_normalized_gradient * standardized_owned, 0),
            jnp.sum(owned_normalized_gradient, 0),
        ),
        "enc",
    )
    return (embeds_recv, hidden_state_gradient, grad_weight, gain_gradient, grad_shift)


def solution(mesh):
    in_specs = (
        P("enc", ("section", "llmdp")),
        P(),
        P(),
        P("enc", ("section", "llmdp")),
        P("enc", None),
        P("enc", ("section", "llmdp")),
    )
    out_specs = (
        P("enc", ("section", "llmdp")),
        P("enc", ("section", "llmdp")),
        P("enc", ("section", "llmdp")),
        P(("section", "llmdp")),
        P(("section", "llmdp")),
    )
    return jax.shard_map(body, mesh=mesh, in_specs=in_specs, out_specs=out_specs, check_vma=False)
```

profile of v0, /device:TPU:28, one launch (start us, length us, event | category | flops | bytes accessed | tf_op | source)
XLA Modules:
  0.0 459.9 jit_solution(16512288865410212296)
XLA Ops:
  7.2 13.7 %all_gather.9 = bf16[512,800]{0,1:T(8,128)(2,1)} all-gather(bf16[256,800]{0,1:T(8,128)(2,1)} %param.6), channel_id=1, replica_groups={{0,4},{8,12},{16,20},{24,28},{1,5},{9,13},{17,21},{25,29},{2,6},{10,14}..., dimensions={0}, use_global_device_ids=true | all-gather | bytes 1228800 | tf_op jit(solution)/shard_map/all_gather | solution.py:38
  22.5 23.0 %all_to_all.90 = bf16[400,2,1024]{2,0,1:T(8,128)(2,1)} all-to-all(bf16[400,2,1024]{2,0,1:T(8,128)(2,1)S(1)} %bitcast.54), channel_id=1, replica_groups={{0,4},{8,12},{16,20},{24,28},{1,5},{9,13},{17,21},{25,29},{2,6},{10,14}..., dimensions={1} | all-to-all | bytes 3276800 | tf_op jit(solution)/shard_map/all_to_all | solution.py:30
  45.5 5.1 %all-to-all-start.3 = ((bf16[8,96,2048]{2,1,0:T(8,128)(2,1)}), bf16[8,96,2048]{2,1,0:T(8,128)(2,1)S(1)}, u32[]{:S(2)}, u32[]{:S(2)}) async-start(bf16[8,96,2048]{2,1,0:T(8,128)(2,1)} %bitcast.58), calls=%async_computation.3 | async-start | bytes 6291456 | tf_op jit(solution)/shard_map/all_to_all | solution.py:59
  51.6 139.8 %all-to-all-done.3 = bf16[8,96,2048]{2,1,0:T(8,128)(2,1)S(1)} async-done(((bf16[8,96,2048]{2,1,0:T(8,128)(2,1)}), bf16[8,96,2048]{2,1,0:T(8,128)(2,1)S(1)}, u32[]{:S(2)}, u32[]{:S(2)}) %all-to-all-start.3) | async-done | bytes 3145760 | tf_op jit(solution)/shard_map/all_to_all | solution.py:59
  191.4 2.3 gather_fusion
  196.0 10.9 %all-to-all-start.4 = ((bf16[256,2,1024]{2,0,1:T(8,128)(2,1)}), bf16[256,2,1024]{2,0,1:T(8,128)(2,1)}, u32[]{:S(2)}, u32[]{:S(2)}) async-start(bf16[256,2,1024]{2,0,1:T(8,128)(2,1)} %bitcast.46), calls=%async_computation.4 | async-start | bytes 2097152 | tf_op jit(solution)/shard_map/all_to_all | solution.py:30
  206.9 3.0 convert_reduce_fusion
  209.9 12.5 %all-to-all-done.4 = bf16[256,2,1024]{2,0,1:T(8,128)(2,1)} async-done(((bf16[256,2,1024]{2,0,1:T(8,128)(2,1)}), bf16[256,2,1024]{2,0,1:T(8,128)(2,1)}, u32[]{:S(2)}, u32[]{:S(2)}) %all-to-all-start.4) | async-done | bytes 1048608 | tf_op jit(solution)/shard_map/all_to_all | solution.py:30
  222.4 7.5 %convolution_convert_fusion = bf16[3200,1024]{1,0:T(8,128)(2,1)} fusion(bf16[512,1024]{1,0:T(8,128)(2,1)} %bitcast.16, bf16[512,3200]{0,1:T(8,128)(2,1)S(1)} %copy-done.2, f32[3200]{0:T(1024)S(1)} %copy-done.8, f32[3200]{0:T(1024)S(1)} %copy-done.7, f32[512]{0:T(512)S(1)} %get-tuple-element.17, f32[512]{0:T(512)S(1)} %get-tuple-element.16), kind=kOutput, calls=%fused_computation.5 | convolution fusion | flops 3368550400 | bytes 10908672 | tf_op jit(solution)/shard_map/dot_general | solution.py:65
  230.0 6.9 %convolution_convert_fusion.1 = bf16[512,3200]{1,0:T(8,128)(2,1)S(1)} fusion(bf16[512,1024]{1,0:T(8,128)(2,1)} %bitcast.16, bf16[3200,1024]{1,0:T(8,128)(2,1)} %all-gather.5.cloned.1.call-done), kind=kOutput, calls=%fused_computation.11 | convolution fusion | flops 3357081600 | bytes 10878976 | tf_op jit(solution)/shard_map/dot_general | solution.py:80
  236.9 3.4 copy.26
  240.3 4.2 all-to-all-start.5
  244.5 8.8 %convolution_convert_fusion.2 = bf16[512,1024]{1,0:T(8,128)(2,1)} fusion(bf16[3200,1024]{1,0:T(8,128)(2,1)} %all-gather.5.cloned.1.call-done, bf16[512,3200]{0,1:T(8,128)(2,1)} %all-gather.3.cloned.1.call-done, f32[3200]{0:T(1024)S(1)} %copy-done.8, f32[3200]{0:T(1024)S(1)} %copy-done.7, f32[512]{0:T(512)S(1)} %get-tuple-element.17, ...), kind=kOutput, calls=%fused_computation.18 | convolution fusion | flops 3365797888 | bytes 10908672 | tf_op jit(solution)/shard_map/dot_general | solution.py:75
  255.6 25.2 %all-to-all-done.5 = bf16[512,4,800]{0,2,1:T(8,128)(2,1)S(1)} async-done(((bf16[512,4,800]{0,2,1:T(8,128)(2,1)}), bf16[512,4,800]{0,2,1:T(8,128)(2,1)S(1)}, u32[]{:S(2)}, u32[]{:S(2)}) %all-to-all-start.5) | async-done | bytes 3276832 | tf_op jit(solution)/shard_map/all_to_all | solution.py:85
  280.8 4.4 all-to-all-start.1
  289.0 11.0 %all-to-all-done.1 = bf16[2,256,1024]{1,2,0:T(8,128)(2,1)} async-done(((bf16[2,256,1024]{1,2,0:T(8,128)(2,1)}), bf16[2,256,1024]{1,2,0:T(8,128)(2,1)}, u32[]{:S(2)}, u32[]{:S(2)}) %all-to-all-start.1) | async-done | bytes 1048608 | tf_op jit(solution)/shard_map/all_to_all | solution.py:30
  300.0 3.5 all-to-all-start.6
  305.0 4.3 scatter_custom_fusion
  309.3 5.5 %all-to-all-done.6 = bf16[2,256,800]{1,2,0:T(8,128)(2,1)S(1)} async-done(((bf16[2,256,800]{1,2,0:T(8,128)(2,1)}), bf16[2,256,800]{1,2,0:T(8,128)(2,1)S(1)}, u32[]{:S(2)}, u32[]{:S(2)}) %all-to-all-start.6) | async-done | bytes 819232 | tf_op jit(solution)/shard_map/all_to_all | solution.py:30
  315.7 5.1 %all-to-all-start.2 = ((bf16[8,96,2048]{2,1,0:T(8,128)(2,1)}), bf16[8,96,2048]{2,1,0:T(8,128)(2,1)S(1)}, u32[]{:S(2)}, u32[]{:S(2)}) async-start(bf16[8,96,2048]{2,1,0:T(8,128)(2,1)} %bitcast.52), calls=%async_computation.2 | async-start | bytes 6291456 | tf_op jit(solution)/shard_map/all_to_all | solution.py:59
  324.9 84.9 %all-to-all-done.2 = bf16[8,96,2048]{2,1,0:T(8,128)(2,1)S(1)} async-done(((bf16[8,96,2048]{2,1,0:T(8,128)(2,1)}), bf16[8,96,2048]{2,1,0:T(8,128)(2,1)S(1)}, u32[]{:S(2)}, u32[]{:S(2)}) %all-to-all-start.2) | async-done | bytes 3145760 | tf_op jit(solution)/shard_map/all_to_all | solution.py:59
  409.8 4.6 %all-to-all-start.7 = ((bf16[2,400,1024]{2,1,0:T(8,128)(2,1)}), bf16[2,400,1024]{2,1,0:T(8,128)(2,1)}, u32[]{:S(2)}, u32[]{:S(2)}) async-start(bf16[2,400,1024]{2,1,0:T(8,128)(2,1)} %bitcast.60), calls=%async_computation.8 | async-start | bytes 3276800 | tf_op jit(solution)/shard_map/all_to_all | solution.py:30
  419.1 7.8 %all-reduce.1 = (f32[256]{0:T(256)}, f32[256]{0:T(256)}) all-reduce(f32[256]{0:T(256)} %get-tuple-element.8, f32[256]{0:T(256)} %get-tuple-element.9), channel_id=1, replica_groups=mesh['enc'=8,'section'=2,'llmdp'=2] {'section','llmdp'}, use_global_device_ids=true, to_apply=%region_11.12 | all-reduce | flops 512 | bytes 4096 | tf_op jit(solution)/shard_map/psum | solution.py:90
  426.8 18.3 %all-reduce = (f32[800]{0:T(1024)}, f32[800]{0:T(1024)}) all-reduce(f32[800]{0:T(1024)} %get-tuple-element.7, f32[800]{0:T(1024)} %get-tuple-element.10), channel_id=1, replica_groups=mesh['enc'=8,'section'=2,'llmdp'=2] {'enc'}, use_global_device_ids=true, to_apply=%region_14.15 | all-reduce | flops 1600 | bytes 12800 | tf_op jit(solution)/shard_map/psum | solution.py:107
  (53 shorter events, 30.3 us)
Async XLA Ops:
  7.2 199.8 %all-gather.3.cloned.1.call-start = ((), (), s32[]{:S(2)}) async-start(), calls=%async_computation.9 | async-start | bytes 4096000 | tf_op jit(solution)/shard_map/all_gather | solution.py:39
  20.9 209.1 %all-gather.5.cloned.1.call-start = ((), (), s32[]{:S(2)}) async-start(), calls=%async_computation.10 | async-start | bytes 8192000 | tf_op jit(solution)/shard_map/all_gather | solution.py:36
  45.5 5.1 %copy-start.4 = (s32[256,1]{0,1:T(1,128)S(1)}, s32[256,1]{0,1:T(1,128)}, u32[]{:S(2)}) copy-start(s32[256,1]{0,1:T(1,128)} %param.10) | copy-start | bytes 3076
  45.5 145.8 %all-to-all-start.3 = ((bf16[8,96,2048]{2,1,0:T(8,128)(2,1)}), bf16[8,96,2048]{2,1,0:T(8,128)(2,1)S(1)}, u32[]{:S(2)}, u32[]{:S(2)}) async-start(bf16[8,96,2048]{2,1,0:T(8,128)(2,1)} %bitcast.58), calls=%async_computation.3 | async-start | bytes 6291456 | tf_op jit(solution)/shard_map/all_to_all | solution.py:59
  193.7 28.7 %copy-start.7 = (f32[3200]{0:T(1024)S(1)}, f32[3200]{0:T(1024)}, u32[]{:S(2)}) copy-start(f32[3200]{0:T(1024)} %param.7) | copy-start | bytes 38404
  193.7 28.7 %copy-start.8 = (f32[3200]{0:T(1024)S(1)}, f32[3200]{0:T(1024)}, u32[]{:S(2)}) copy-start(f32[3200]{0:T(1024)} %param.8) | copy-start | bytes 38404
  196.0 26.4 %all-to-all-start.4 = ((bf16[256,2,1024]{2,0,1:T(8,128)(2,1)}), bf16[256,2,1024]{2,0,1:T(8,128)(2,1)}, u32[]{:S(2)}, u32[]{:S(2)}) async-start(bf16[256,2,1024]{2,0,1:T(8,128)(2,1)} %bitcast.46), calls=%async_computation.4 | async-start | bytes 2097152 | tf_op jit(solution)/shard_map/all_to_all | solution.py:30
  206.9 202.9 %reduce-scatter.2.cloned.1.call-start = ((), (), s32[]{:S(2)}) async-start(), calls=%async_computation.11 | async-start | bytes 8192000 | tf_op jit(solution)/shard_map/reduce_scatter | solution.py:64
  206.9 15.5 %copy-start.2 = (bf16[512,3200]{0,1:T(8,128)(2,1)S(1)}, bf16[512,3200]{0,1:T(8,128)(2,1)}, u32[]{:S(2)}) copy-start(bf16[512,3200]{0,1:T(8,128)(2,1)} %all-gather.3.cloned.1.call-done) | copy-start | bytes 9830404
  209.9 34.6 %copy-start.5 = (f32[512]{0:T(512)}, f32[512]{0:T(512)S(1)}, u32[]{:S(2)}) copy-start(f32[512]{0:T(512)S(1)} %get-tuple-element.17) | copy-start | bytes 6148
  209.9 34.6 %copy-start.6 = (f32[512]{0:T(512)}, f32[512]{0:T(512)S(1)}, u32[]{:S(2)}) copy-start(f32[512]{0:T(512)S(1)} %get-tuple-element.16) | copy-start | bytes 6148
  240.3 40.5 %all-to-all-start.5 = ((bf16[512,4,800]{0,2,1:T(8,128)(2,1)}), bf16[512,4,800]{0,2,1:T(8,128)(2,1)S(1)}, u32[]{:S(2)}, u32[]{:S(2)}) async-start(bf16[512,4,800]{0,2,1:T(8,128)(2,1)} %bitcast.50), calls=%async_computation.5 | async-start | bytes 6553600 | tf_op jit(solution)/shard_map/all_to_all | solution.py:85
  280.8 19.1 %all-to-all-start.1 = ((bf16[2,256,1024]{1,2,0:T(8,128)(2,1)}), bf16[2,256,1024]{1,2,0:T(8,128)(2,1)}, u32[]{:S(2)}, u32[]{:S(2)}) async-start(bf16[2,256,1024]{1,2,0:T(8,128)(2,1)} %copy.23), calls=%async_computation.1 | async-start | bytes 2097152 | tf_op jit(solution)/shard_map/all_to_all | solution.py:30
  300.0 14.9 %all-to-all-start.6 = ((bf16[2,256,800]{1,2,0:T(8,128)(2,1)}), bf16[2,256,800]{1,2,0:T(8,128)(2,1)S(1)}, u32[]{:S(2)}, u32[]{:S(2)}) async-start(bf16[2,256,800]{1,2,0:T(8,128)(2,1)} %bitcast.47), calls=%async_computation.6 | async-start | bytes 1638400 | tf_op jit(solution)/shard_map/all_to_all | solution.py:30
  314.8 0.9 copy-start.3
  315.7 94.1 %all-to-all-start.2 = ((bf16[8,96,2048]{2,1,0:T(8,128)(2,1)}), bf16[8,96,2048]{2,1,0:T(8,128)(2,1)S(1)}, u32[]{:S(2)}, u32[]{:S(2)}) async-start(bf16[8,96,2048]{2,1,0:T(8,128)(2,1)} %bitcast.52), calls=%async_computation.2 | async-start | bytes 6291456 | tf_op jit(solution)/shard_map/all_to_all | solution.py:59
  320.8 96.6 %copy-start.1 = (bf16[256,800]{0,1:T(8,128)(2,1)S(1)}, bf16[256,800]{0,1:T(8,128)(2,1)}, u32[]{:S(2)}) copy-start(bf16[256,800]{0,1:T(8,128)(2,1)} %param.6) | copy-start | bytes 1228804
  409.8 38.1 %all-to-all-start.7 = ((bf16[2,400,1024]{2,1,0:T(8,128)(2,1)}), bf16[2,400,1024]{2,1,0:T(8,128)(2,1)}, u32[]{:S(2)}, u32[]{:S(2)}) async-start(bf16[2,400,1024]{2,1,0:T(8,128)(2,1)} %bitcast.60), calls=%async_computation.8 | async-start | bytes 3276800 | tf_op jit(solution)/shard_map/all_to_all | solution.py:30
  416.5 0.9 copy-start
Sparse Core Ops, SparseCore 0:
  21.0 28.3 all-gather.2
  51.0 172.6 all-gather.4
  230.1 136.1 reduce-scatter.1
where the time goes:
time: 468 us; the launch traced here: 460 us
  waiting for transfers between devices  279 us (60%)
  blocking collectives  62.7 us (13%)
  starting transfers between devices  38 us (8%)
  local copies, waits for them, and re-layouts  29.5 us (6%)
  matrix products  23.2 us (5%)
  between operations  13.9 us (3%)
  other arithmetic  13.7 us (3%)
    all_to_all x2, waiting for transfers between devices, enc_exchange(): lax.all_to_all(x.reshape(senders, most_slots, out_cols), 'enc', split_axi...  225 us
    all_to_all x4, waiting for transfers between devices, near_exchange(): lax.all_to_all(x, 'enc', split, concat, axis_index_groups=near, tiled=True)  29 us
    all_to_all x1, waiting for transfers between devices, body(): lax.all_to_all(pieces, features, split_axis=1, concat_axis=1, tiled=True)  25.2 us
    all_to_all x4, starting transfers between devices, near_exchange(): lax.all_to_all(x, 'enc', split, concat, axis_index_groups=near, tiled=True)  23.5 us
    all_to_all x1, blocking collectives, near_exchange(): lax.all_to_all(x, 'enc', split, concat, axis_index_groups=near, tiled=True)  23 us
    psum x1, blocking collectives, body(): lax.psum((jnp.sum(owned_normalized_gradient * standardized_owned, 0), jnp...  18.3 us
    all_gather x1, blocking collectives, body(): lax.all_gather(patches, 'enc', axis=0, axis_index_groups=near, tiled=True)  13.7 us
    all_to_all x2, starting transfers between devices, enc_exchange(): lax.all_to_all(x.reshape(senders, most_slots, out_cols), 'enc', split_axi...  10.2 us
  transfers between devices with their start and end apart: 10, of which 6 were waited for; matrix products, arithmetic and copies ran while one was open for 13% of the time, Pallas kernels for 0%

commit v1 on v0

--- a/solution.py
+++ b/solution.py
@@ -1,12 +1,20 @@
+import functools
+
 import jax
 import jax.numpy as jnp
 from jax import lax
+from jax.experimental import pallas as pl
+from jax.experimental.pallas import tpu as pltpu
 from jax.sharding import PartitionSpec as P
 
 EPSILON = 1e-05
-
+MESH = pl.DeviceIdType.MESH
+F32 = jnp.float32
+BF16 = jnp.bfloat16
 
 MAX_BLOCK = 2
+SUBLANES = 16
+LANES = 128
 
 
 def block_size(senders, out_cols):
@@ -16,7 +24,452 @@
     return size
 
 
-def body(patches, gain, shift, proj_weight, llm_rank, embed_grad):
+def slots_of(llm_rank, senders, most_slots):
+    target = llm_rank[:, 0]
+    owners = jnp.arange(senders, dtype=jnp.int32)
+    hits = (target[:, None] == owners[None, :]).astype(jnp.int32)
+    rank = jnp.sum((jnp.cumsum(hits, 0) - hits) * hits, 1)
+    return target * most_slots + rank
+
+
+class Place:
+    def __init__(self):
+        self.e = lax.axis_index("enc")
+        self.k = lax.axis_index("section")
+        self.y = lax.axis_index("llmdp")
+        self.x = lax.rem(self.e, 2)
+        self.senders = lax.axis_size("enc")
+        self.c = self.group(self.k, self.y)
+        self.x_peer = (self.e + 1 - 2 * self.x, self.k, self.y)
+        self.y_peer = (self.e, self.k, 1 - self.y)
+        self.k_peer = (self.e, 1 - self.k, self.y)
+
+    def group(self, k, y):
+        return k * 2 + y
+
+    def other(self, step):
+        return lax.rem(self.e + step, self.senders)
+
+    def greet(self):
+        barrier = pltpu.get_barrier_semaphore()
+
+        def one(step, carry):
+            pl.semaphore_signal(
+                barrier, inc=1, device_id=(self.other(step), self.k, self.y), device_id_type=MESH
+            )
+            return carry
+
+        lax.fori_loop(1, self.senders, one, 0)
+        for peer in (self.y_peer, self.k_peer):
+            pl.semaphore_signal(barrier, inc=1, device_id=peer, device_id_type=MESH)
+        pl.semaphore_wait(barrier, self.senders + 1)
+
+
+def send(src, dst, send_sem, recv_sem, device):
+    return pltpu.make_async_remote_copy(
+        src_ref=src, dst_ref=dst, send_sem=send_sem, recv_sem=recv_sem, device_id=device, device_id_type=MESH
+    )
+
+
+def spread_kernel(
+    out_ref, eg_ref, gw_ref, n_ref, eg_out,
+    nv, eg_v, route_s, route_r, x_s, x_r, y_s, y_r, d_s, d_r, eg_sem, local_sem, n_sem,
+):
+    at = Place()
+    senders, most, width = out_ref.shape
+    half = eg_v.shape[2]
+    rows = eg_v.shape[1]
+    e, k, y, x, c = at.e, at.k, at.y, at.x, at.c
+    ox = 1 - x
+    c_y, c_k, c_ky = at.group(k, 1 - y), at.group(1 - k, y), at.group(1 - k, 1 - y)
+
+    def route(d):
+        return send(out_ref.at[d], nv.at[c, lax.rem(d, 2), e], route_s.at[d], route_r.at[e], (d, k, y))
+
+    def route_in(s):
+        return send(out_ref.at[s], nv.at[c, x, s], route_s.at[s], route_r.at[s], (s, k, y))
+
+    def x_hop(s, src):
+        return send(src, nv.at[c, x, s], x_s.at[s], x_r.at[s], at.x_peer)
+
+    def x_in(s):
+        return send(nv.at[c, ox, s], nv.at[c, ox, s], x_s.at[s], x_r.at[s], at.x_peer)
+
+    def y_hop(w, s, src):
+        return send(src, nv.at[c, w, s], y_s.at[w, s], y_r.at[w, s], at.y_peer)
+
+    def y_in(w, s):
+        return send(nv.at[c_y, w, s], nv.at[c_y, w, s], y_s.at[w, s], y_r.at[w, s], at.y_peer)
+
+    def k_hop(v, w, s, src):
+        return send(src, nv.at[at.group(k, v), w, s], d_s.at[v, w, s], d_r.at[v, w, s], at.k_peer)
+
+    def k_in(v, w, s):
+        ref = nv.at[at.group(1 - k, v), w, s]
+        return send(ref, ref, d_s.at[v, w, s], d_r.at[v, w, s], at.k_peer)
+
+    eg_send = send(
+        eg_ref.at[:, pl.ds(pl.multiple_of(ox * half, LANES), half)], eg_v.at[x], eg_sem.at[0], eg_sem.at[1], at.x_peer
+    )
+    eg_load = pltpu.make_async_copy(
+        eg_ref.at[:, pl.ds(pl.multiple_of(x * half, LANES), half)], eg_v.at[x], local_sem.at[0]
+    )
+    eg_in = send(eg_v.at[ox], eg_v.at[ox], eg_sem.at[0], eg_sem.at[1], at.x_peer)
+
+    eg_load.start()
+    at.greet()
+
+    def over(fn, start=0):
+        lax.fori_loop(start, senders, lambda i, carry: (fn(i), carry)[1], 0)
+
+    over(lambda step: route(at.other(step)).start(), 1)
+    own = out_ref.at[e]
+    x_hop(e, own).start()
+    y_hop(x, e, own).start()
+    k_hop(y, x, e, own).start()
+    nv[c, x, e] = out_ref[e]
+
+    def pass_on(step):
+        s = at.other(step)
+        ref = nv.at[c, x, s]
+        route_in(s).wait_recv()
+        x_hop(s, ref).start()
+        y_hop(x, s, ref).start()
+        k_hop(y, x, s, ref).start()
+
+    over(pass_on, 1)
+    eg_send.start()
+
+    def pass_x(step):
+        s = at.other(step)
+        ref = nv.at[c, ox, s]
+        x_in(s).wait_recv()
+        y_hop(ox, s, ref).start()
+        k_hop(y, ox, s, ref).start()
+
+    over(pass_x)
+
+    def product(group):
+        total = None
+        for w in range(2):
+            term = lax.dot_general(
+                nv[group, w].reshape(rows, width), eg_v[w], (((0,), (0,)), ((), ())), preferred_element_type=F32
+            )
+            total = term if total is None else total + term
+        gw_ref[pl.ds(pl.multiple_of(group * width, SUBLANES), width), :] = total.astype(BF16)
+
+    def keep(i, group):
+        pltpu.make_async_copy(nv.at[group], n_ref.at[group], n_sem.at[i]).start()
+
+    def pass_y(w):
+        def one(step):
+            s = at.other(step)
+            y_in(w, s).wait_recv()
+            k_hop(1 - y, w, s, nv.at[c_y, w, s]).start()
+
+        over(one)
+
+    keep(0, c)
+    eg_load.wait()
+    eg_in.wait_recv()
+    eg_keep = pltpu.make_async_copy(eg_v, eg_out, local_sem.at[0])
+    eg_keep.start()
+    product(c)
+    pass_y(x)
+
+    def near_in(step):
+        for w in range(2):
+            k_in(y, w, at.other(step)).wait_recv()
+
+    over(near_in)
+    keep(1, c_k)
+    product(c_k)
+    pass_y(ox)
+    keep(2, c_y)
+    product(c_y)
+
+    def far_in(step):
+        for w in range(2):
+            k_in(1 - y, w, at.other(step)).wait_recv()
+
+    over(far_in)
+    keep(3, c_ky)
+    product(c_ky)
+
+    over(lambda step: route(at.other(step)).wait_send(), 1)
+
+    def sent(step):
+        s = at.other(step)
+        x_hop(s, nv.at[c, x, s]).wait_send()
+        for w in range(2):
+            y_hop(w, s, nv.at[c, w, s]).wait_send()
+            for v in range(2):
+                k_hop(v, w, s, nv.at[at.group(k, v), w, s]).wait_send()
+
+    over(sent)
+    eg_send.wait_send()
+    eg_keep.wait()
+    for i, group in enumerate((c, c_k, c_y, c_ky)):
+        pltpu.make_async_copy(nv.at[group], n_ref.at[group], n_sem.at[i]).wait()
+
+
+def spread(outgoing, embed_grad):
+    senders, most, width = outgoing.shape
+    groups = 4
+    rows, cols = embed_grad.shape
+    half = cols // 2
+    dma = pltpu.SemaphoreType.DMA
+    any_spec = pl.BlockSpec(memory_space=pl.ANY)
+    vmem = pl.BlockSpec(memory_space=pltpu.VMEM)
+    return pl.pallas_call(
+        spread_kernel,
+        out_shape=(
+            jax.ShapeDtypeStruct((groups * width, half), BF16),
+            jax.ShapeDtypeStruct((groups, 2, senders, most, width), BF16),
+            jax.ShapeDtypeStruct((2, rows, half), BF16),
+        ),
+        in_specs=[vmem, any_spec],
+        out_specs=(vmem, any_spec, any_spec),
+        scratch_shapes=[
+            pltpu.VMEM((groups, 2, senders, most, width), BF16),
+            pltpu.VMEM((2, rows, half), BF16),
+            dma((senders,)), dma((senders,)), dma((senders,)), dma((senders,)),
+            dma((2, senders)), dma((2, senders)), dma((2, 2, senders)), dma((2, 2, senders)),
+            dma((2,)), dma((1,)), dma((groups,)),
+        ],
+        compiler_params=pltpu.CompilerParams(
+            collective_id=0, has_side_effects=True, vmem_limit_bytes=56 * 1024 * 1024
+        ),
+        cost_estimate=pl.CostEstimate(
+            flops=60 * 10**9, bytes_accessed=32 * rows * half, transcendentals=0
+        ),
+        name="spread",
+    )(outgoing, embed_grad)
+
+
+def finish_kernel(
+    n_ref, w_ref, eg_ref, emb_ref, t_ref,
+    nv, dv, ra, yb, xb, rb, ev, a_s, a_r, b_s, b_r, c_s, c_r, t_s, t_r, e_sem, n_sem, l_sem,
+):
+    at = Place()
+    senders, most, width = t_ref.shape
+    rows, half = eg_ref.shape[1:]
+    e, k, y, x, c = at.e, at.k, at.y, at.x, at.c
+    ox, oy, ok = 1 - x, 1 - y, 1 - k
+    c_y = at.group(k, oy)
+
+    def load(w):
+        return pltpu.make_async_copy(n_ref.at[:, w], nv, n_sem.at[0])
+
+    load(ox).start()
+    at.greet()
+
+    def over(fn):
+        lax.fori_loop(0, senders, lambda i, carry: (fn(i), carry)[1], 0)
+
+    def product(group):
+        for w in range(2):
+            total = lax.dot_general(
+                eg_ref[w], w_ref[group], (((1,), (1,)), ((), ())), preferred_element_type=F32
+            )
+            dv[group, w] = total.astype(BF16).reshape(senders, most, width)
+
+    def core(v, s):
+        return send(
+            dv.at[at.group(ok, v), :, s], ra.at[v, :, s], a_s.at[v, s], a_r.at[v, s], at.k_peer
+        )
+
+    product(at.group(ok, oy))
+    over(lambda s: core(oy, s).start())
+    product(c_y)
+
+    def across(s):
+        return send(dv.at[c_y, :, s], yb.at[:, s], b_s.at[s], b_r.at[s], at.y_peer)
+
+    def fold_core(s):
+        core(oy, s).wait_recv()
+        dv[c_y, :, s] = (dv[c_y, :, s].astype(F32) + ra[oy, :, s].astype(F32)).astype(BF16)
+        across(s).start()
+
+    over(fold_core)
+    product(at.group(ok, y))
+    over(lambda s: core(y, s).start())
+    product(c)
+
+    def embed(w):
+        total = None
+        for group in range(w_ref.shape[0]):
+            term = jnp.dot(
+                nv[group].reshape(rows, width), w_ref[group], preferred_element_type=F32
+            )
+            total = term if total is None else total + term
+        return total.astype(BF16)
+
+    own_cols = pl.ds(pl.multiple_of(x * half, LANES), half)
+    load(ox).wait()
+    ev[0] = embed(ox)
+    load(x).start()
+    emb_send = send(ev.at[0], emb_ref.at[:, own_cols], e_sem.at[0], e_sem.at[1], at.x_peer)
+
+    def to_x(s):
+        return send(dv.at[c, ox, s], xb.at[s], c_s.at[s], c_r.at[s], at.x_peer)
+
+    def fold_y(s):
+        core(y, s).wait_recv()
+        across(s).wait_recv()
+        dv[c, :, s] = (
+            dv[c, :, s].astype(F32) + ra[y, :, s].astype(F32) + yb[:, s].astype(F32)
+        ).astype(BF16)
+        to_x(s).start()
+
+    def back(s):
+        return send(rb.at[s], t_ref.at[e], t_s.at[s], t_r.at[e], (s, k, y))
+
+    def fold_x(s):
+        to_x(s).wait_recv()
+        rb[s] = (dv[c, x, s].astype(F32) + xb[s].astype(F32)).astype(BF16)
+
+        @pl.when(s == e)
+        def _():
+            t_ref[e] = rb[e]
+
+        @pl.when(s != e)
+        def _():
+            back(s).start()
+
+    load(x).wait()
+    ev[1] = embed(x)
+    keep = pltpu.make_async_copy(ev.at[1], emb_ref.at[:, own_cols], l_sem.at[0])
+    keep.start()
+
+    fold_y(0)
+    emb_send.start()
+
+    def step(s):
+        fold_y(s)
+        fold_x(s - 1)
+
+    lax.fori_loop(1, senders, lambda i, carry: (step(i), carry)[1], 0)
+    fold_x(senders - 1)
+
+    def came(i):
+        s = at.other(i)
+        send(rb.at[s], t_ref.at[s], t_s.at[s], t_r.at[s], (s, k, y)).wait_recv()
+        back(s).wait_send()
+
+    lax.fori_loop(1, senders, lambda i, carry: (came(i), carry)[1], 0)
+
+    def sent(s):
+        core(oy, s).wait_send()
+        core(y, s).wait_send()
+        across(s).wait_send()
+        to_x(s).wait_send()
+
+    over(sent)
+    emb_send.wait_send()
+    send(
+        ev.at[0], emb_ref.at[:, pl.ds(pl.multiple_of(ox * half, LANES), half)], e_sem.at[0], e_sem.at[1], at.x_peer
+    ).wait_recv()
+    keep.wait()
+
+
+def finish(shared, weight, grads):
+    groups, _, senders, most, width = shared.shape
+    _, rows, half = grads.shape
+    dma = pltpu.SemaphoreType.DMA
+    any_spec = pl.BlockSpec(memory_space=pl.ANY)
+    vmem = pl.BlockSpec(memory_space=pltpu.VMEM)
+    return pl.pallas_call(
+        finish_kernel,
+        out_shape=(
+            jax.ShapeDtypeStruct((rows, 2 * half), BF16),
+            jax.ShapeDtypeStruct((senders, most, width), BF16),
+        ),
+        in_specs=[any_spec, vmem, vmem],
+        out_specs=(any_spec, vmem),
+        scratch_shapes=[
+            pltpu.VMEM((groups, senders, most, width), BF16),
+            pltpu.VMEM((groups, 2, senders, most, width), BF16),
+            pltpu.VMEM((2, 2, senders, most, width), BF16),
+            pltpu.VMEM((2, senders, most, width), BF16),
+            pltpu.VMEM((senders, most, width), BF16),
+            pltpu.VMEM((senders, most, width), BF16),
+            pltpu.VMEM((2, rows, half), BF16),
+            dma((2, senders)), dma((2, senders)), dma((senders,)), dma((senders,)),
+            dma((senders,)), dma((senders,)), dma((senders,)), dma((senders,)),
+            dma((2,)), dma((1,)), dma((1,)),
+        ],
+        compiler_params=pltpu.CompilerParams(
+            collective_id=1, has_side_effects=True, vmem_limit_bytes=62 * 1024 * 1024
+        ),
+        cost_estimate=pl.CostEstimate(
+            flops=60 * 10**9, bytes_accessed=32 * rows * half, transcendentals=0
+        ),
+        name="finish",
+    )(shared, weight, grads)
+
+
+def owner_body(patches, gain, shift, proj_weight, llm_rank, embed_grad):
+    features = ("section", "llmdp")
+    own_rows, owned_width = patches.shape
+    width = gain.shape[0]
+    senders = lax.axis_size("enc")
+    most_slots = embed_grad.shape[0] // senders
+    block = 2
+    near = [[b * block + i for i in range(block)] for b in range(senders // block)]
+    far = [[b * block + i for b in range(senders // block)] for i in range(block)]
+
+    def near_exchange(v, split, concat):
+        return lax.all_to_all(v, "enc", split, concat, axis_index_groups=near, tiled=True)
+
+    weight_part = near_exchange(proj_weight, 1, 0)
+    weight = lax.all_gather(weight_part, "enc", axis=0, axis_index_groups=far, tiled=True)
+
+    column_start = lax.axis_index(features) * owned_width
+    gain_own = lax.dynamic_slice_in_dim(gain, column_start, owned_width, 0)
+    shift_own = lax.dynamic_slice_in_dim(shift, column_start, owned_width, 0)
+    values = patches.astype(F32)
+    total, squares = lax.psum((jnp.sum(values, 1), jnp.sum(values * values, 1)), features)
+    average = (total / width)[:, None]
+    variance = (squares / width)[:, None] - average * average
+    deviation = lax.rsqrt(variance + EPSILON)
+    standardized = (values - average) * deviation
+    normed = (standardized * gain_own + shift_own).astype(BF16)
+
+    slot = slots_of(llm_rank, senders, most_slots)
+    places = jnp.arange(senders * most_slots, dtype=jnp.int32)
+    chosen = (places[:, None] == slot[None, :]).astype(BF16)
+    outgoing = jnp.dot(chosen, normed, preferred_element_type=F32).astype(BF16)
+    grad_partial, shared, grads = spread(
+        outgoing.reshape(senders, most_slots, owned_width), embed_grad
+    )
+    grad_part = lax.psum_scatter(
+        grad_partial, "enc", scatter_dimension=0, axis_index_groups=far, tiled=True
+    )
+    grad_weight = near_exchange(grad_part, 0, 1).astype(F32)
+
+    embeds_recv, returned = finish(
+        shared, weight.reshape(width // owned_width, owned_width, weight.shape[1]), grads
+    )
+    dnormed = lax.dot_general(
+        chosen, returned.reshape(senders * most_slots, owned_width), (((0,), (0,)), ((), ())),
+        preferred_element_type=F32,
+    )
+    dxhat = dnormed * gain_own
+    mean_sum, cross_sum = lax.psum(
+        (jnp.sum(dxhat, 1), jnp.sum(dxhat * standardized, 1)), features
+    )
+    hidden_state_gradient = (
+        deviation
+        * (dxhat - (mean_sum / width)[:, None] - standardized * (cross_sum / width)[:, None])
+    ).astype(BF16)
+    gain_gradient, grad_shift = lax.psum(
+        (jnp.sum(dnormed * standardized, 0), jnp.sum(dnormed, 0)), "enc"
+    )
+    return (embeds_recv, hidden_state_gradient, grad_weight, gain_gradient, grad_shift)
+
+
+def plain_body(patches, gain, shift, proj_weight, llm_rank, embed_grad):
     features = ("section", "llmdp")
     own_rows, owned_width = patches.shape
     width = gain.shape[0]
@@ -114,6 +567,25 @@
     return (embeds_recv, hidden_state_gradient, grad_weight, gain_gradient, grad_shift)
 
 
+def fits(patches, gain, proj_weight, embed_grad):
+    senders, cores, rows_of = (lax.axis_size(a) for a in ("enc", "section", "llmdp"))
+    most = embed_grad.shape[0] // senders
+    return (
+        cores == 2
+        and rows_of == 2
+        and block_size(senders, proj_weight.shape[1]) == 2
+        and senders // 2 == cores * rows_of
+        and most % SUBLANES == 0
+        and proj_weight.shape[0] % SUBLANES == 0
+        and patches.shape[1] == 2 * proj_weight.shape[0]
+    )
+
+
+def body(patches, gain, shift, proj_weight, llm_rank, embed_grad):
+    form = owner_body if fits(patches, gain, proj_weight, embed_grad) else plain_body
+    return form(patches, gain, shift, proj_weight, llm_rank, embed_grad)
+
+
 def solution(mesh):
     in_specs = (
         P("enc", ("section", "llmdp")),

time: 468 us -> 557 us (1.19)
  Pallas kernels: 0 us -> 243 us
  waiting for transfers between devices: 279 us -> 211 us
  starting transfers between devices: 38 us -> 3.94 us
  local copies, waits for them, and re-layouts: 29.5 us -> 9.55 us
  matrix products: 23.2 us -> 4.08 us
  other arithmetic: 13.7 us -> 5.29 us
    all_to_all x7 -> x1, waiting for transfers between devices: 279 us -> 0.01 us  [near_exchange(): lax.all_to_all(v, 'enc', split, concat, axis_index_groups=near, tiled=True)]
    pallas_call x0 -> x2, Pallas kernels: none -> 243 us  [the longest x1 138 us: finish(): pl.pallas_call(finish_kernel, out_shape=(jax.ShapeDtypeStruct((rows, 2 *...]
    all_gather x2 -> x1, waiting for transfers between devices: 0.02 us -> 116 us  [owner_body(): lax.all_gather(weight_part, 'enc', axis=0, axis_index_groups=far, tiled=T...]
    reduce_scatter x1, waiting for transfers between devices: 0.01 us -> 95 us  [owner_body(): lax.psum_scatter(grad_partial, 'enc', scatter_dimension=0, axis_index_gro...]
    all_to_all x7 -> x1, starting transfers between devices: 37.9 us -> 3.86 us  [near_exchange(): lax.all_to_all(v, 'enc', split, concat, axis_index_groups=near, tiled=True)]
    dot_general x3 -> x2, matrix products: 23.2 us -> 4.08 us  [the longest x1 2.44 us: owner_body(): lax.dot_general(chosen, returned.reshape(senders * most_slots, owned_widt...]
    all_gather x1 -> x0, blocking collectives: 13.7 us -> none  [body(): lax.all_gather(patches, 'enc', axis=0, axis_index_groups=near, tiled=True)]
    psum x2 -> x3, blocking collectives: 26 us -> 35.1 us  [the longest x1 20.9 us: owner_body(): lax.psum((jnp.sum(dnormed * standardized, 0), jnp.sum(dnormed, 0)), 'enc')]
  transfers between devices with their start and end apart: 10 -> 3, of which waited for: 6 -> 2; matrix products, arithmetic and copies ran while one was open for 13% -> 1% of each run, Pallas kernels for 0% -> 25%
where the time goes in v1:
time: 557 us; the launch traced here: 549 us
  Pallas kernels  243 us (44%)
  waiting for transfers between devices  211 us (38%)
  blocking collectives  59 us (11%)
  between operations  14.1 us (3%)
  local copies, waits for them, and re-layouts  9.55 us (2%)
    pallas_call x1, Pallas kernels, finish(): pl.pallas_call(finish_kernel, out_shape=(jax.ShapeDtypeStruct((rows, 2 *...  138 us
    all_gather x1, waiting for transfers between devices, owner_body(): lax.all_gather(weight_part, 'enc', axis=0, axis_index_groups=far, tiled=T...  116 us
    pallas_call x1, Pallas kernels, spread(): pl.pallas_call(spread_kernel, out_shape=(jax.ShapeDtypeStruct((groups * w...  105 us
    reduce_scatter x1, waiting for transfers between devices, owner_body(): lax.psum_scatter(grad_partial, 'enc', scatter_dimension=0, axis_index_gro...  95 us
    all_to_all x1, blocking collectives, near_exchange(): lax.all_to_all(v, 'enc', split, concat, axis_index_groups=near, tiled=True)  23.9 us
    psum x1, blocking collectives, owner_body(): lax.psum((jnp.sum(dnormed * standardized, 0), jnp.sum(dnormed, 0)), 'enc')  20.9 us
  transfers between devices with their start and end apart: 3, of which 2 were waited for; matrix products, arithmetic and copies ran while one was open for 1% of the time, Pallas kernels for 25%

profile of v1, /device:TPU:28, one launch (start us, length us, event | category | flops | bytes accessed | tf_op | source)
XLA Modules:
  0.0 549.4 jit_solution(4480472472401103585)
XLA Ops:
  7.2 1.2 convert_reduce_fusion
  8.4 0.8 dynamic_slice.6
  9.2 0.8 dynamic_slice.7
  9.9 0.7 fusion.23
  10.6 0.6 reduce-window.6
  11.4 0.8 fusion.22
  12.2 0.7 multiply_add_fusion
  12.9 7.0 %all-reduce.2 = (f32[256]{0:T(256)S(1)}, f32[256]{0:T(256)S(1)}) all-reduce(f32[256]{0:T(256)S(1)} %get-tuple-element.20, f32[256]{0:T(256)S(1)} %get-tuple-element.19), channel_id=1, replica_groups=mesh['enc'=8,'section'=2,'llmdp'=2] {'section','llmdp'}, use_global_device_ids=true, to_apply=%region_6.7 | all-reduce | flops 512 | bytes 4096 | tf_op jit(solution)/shard_map/psum | solution.py:432
  19.9 1.6 convolution_convert_fusion
  21.6 1.6 copy.19
  23.1 105.1 %spread.1 = (bf16[3200,1024]{1,0:T(8,128)(2,1)}, bf16[4,2,8,96,800]{4,3,2,1,0:T(8,128)(2,1)}, bf16[2,768,1024]{2,1,0:T(8,128)(2,1)}) custom-call(bf16[8,96,800]{2,1,0:T(8,128)(2,1)} %bitcast.31, bf16[768,2048]{1,0:T(8,128)(2,1)} %eg_ref.1), custom_call_target="tpu_custom_call" | custom-call | flops 60000002048 | bytes 25165824 | tf_op jit(solution)/shard_map/spread/pallas_call | solution.py:224
  128.3 1.3 copy-done.1
  129.8 23.9 %all_to_all.32 = bf16[400,2,1024]{2,0,1:T(8,128)(2,1)} all-to-all(bf16[400,2,1024]{2,0,1:T(8,128)(2,1)S(1)} %bitcast.27), channel_id=1, replica_groups={{0,4},{8,12},{16,20},{24,28},{1,5},{9,13},{17,21},{25,29},{2,6},{10,14}..., dimensions={1} | all-to-all | bytes 3276800 | tf_op jit(solution)/shard_map/all_to_all | solution.py:423
  153.7 95.0 %reduce-scatter.2.cloned.1.call-done = bf16[800,1024]{1,0:T(8,128)(2,1)} async-done(((bf16[3200,1024]{1,0:T(8,128)(2,1)}), bf16[800,1024]{1,0:T(8,128)(2,1)}) %reduce-scatter.2.cloned.1.call-update) | async-done | bytes 1638416 | tf_op jit(solution)/shard_map/reduce_scatter | solution.py:446
  248.7 3.9 all-to-all-start.1
  252.6 115.5 %all-gather.2.cloned.1.call-done = bf16[3200,1024]{1,0:T(8,128)(2,1)} async-done(((bf16[800,1024]{1,0:T(8,128)(2,1)}), bf16[3200,1024]{1,0:T(8,128)(2,1)}) %all-gather.2.cloned.1.call-update) | async-done | bytes 6553616 | tf_op jit(solution)/shard_map/all_gather | solution.py:426
  368.1 137.7 %finish.1 = (bf16[768,2048]{1,0:T(8,128)(2,1)}, bf16[8,96,800]{2,1,0:T(8,128)(2,1)}) custom-call(bf16[4,2,8,96,800]{4,3,2,1,0:T(8,128)(2,1)} %get-tuple-element.10.n_ref, bf16[4,800,1024]{2,1,0:T(8,128)(2,1)} %bitcast.35, bf16[2,768,1024]{2,1,0:T(8,128)(2,1)} %get-tuple-element.11.eg_ref), custom_call_target="tpu_custom_call" | custom-call | flops 60000002048 | bytes 25165824 | tf_op jit(solution)/shard_map/finish/pallas_call | solution.py:382
  505.9 2.4 fusion.11
  508.3 7.2 %all-reduce.1 = (f32[256]{0:T(256)S(1)}, f32[256]{0:T(256)S(1)}) all-reduce(f32[256]{0:T(256)S(1)} %get-tuple-element.16, f32[256]{0:T(256)S(1)} %get-tuple-element.17), channel_id=1, replica_groups=mesh['enc'=8,'section'=2,'llmdp'=2] {'section','llmdp'}, use_global_device_ids=true, to_apply=%region_10.11 | all-reduce | flops 512 | bytes 4096 | tf_op jit(solution)/shard_map/psum | solution.py:459
  515.5 20.9 %all-reduce = (f32[800]{0:T(1024)}, f32[800]{0:T(1024)}) all-reduce(f32[800]{0:T(1024)S(1)} %get-tuple-element.15, f32[800]{0:T(1024)S(1)} %get-tuple-element.18), channel_id=1, replica_groups=mesh['enc'=8,'section'=2,'llmdp'=2] {'enc'}, use_global_device_ids=true, to_apply=%region_13.14 | all-reduce | flops 1600 | bytes 12800 | tf_op jit(solution)/shard_map/psum | solution.py:466
  536.4 1.0 fusion.10
  537.8 1.9 copy.23
  539.7 1.1 copy-done
  540.9 1.7 copy.27
  (16 shorter events, 0.9 us)
Async XLA Ops:
  7.2 241.6 %reduce-scatter.2.cloned.1.call-start = ((), (), s32[]{:S(2)}) async-start(), calls=%async_computation.4 | async-start | bytes 8192000 | tf_op jit(solution)/shard_map/reduce_scatter | solution.py:446
  128.2 1.4 copy-start.1
  128.3 239.9 %all-gather.2.cloned.1.call-start = ((), (), s32[]{:S(2)}) async-start(), calls=%async_computation.3 | async-start | bytes 8192000 | tf_op jit(solution)/shard_map/all_gather | solution.py:426
  248.7 288.6 %all-to-all-start.1 = ((bf16[2,400,1024]{2,1,0:T(8,128)(2,1)}), bf16[2,400,1024]{2,1,0:T(8,128)(2,1)S(1)}, u32[]{:S(2)}, u32[]{:S(2)}) async-start(bf16[2,400,1024]{2,1,0:T(8,128)(2,1)} %bitcast.30), calls=%async_computation.2 | async-start | bytes 3276800 | tf_op jit(solution)/shard_map/all_to_all | solution.py:423
  505.9 30.5 %copy-start.2 = (bf16[256,800]{0,1:T(8,128)(2,1)S(1)}, bf16[256,800]{0,1:T(8,128)(2,1)}, u32[]{:S(2)}) copy-start(bf16[256,800]{0,1:T(8,128)(2,1)} %param.6) | copy-start | bytes 1228804
  537.8 3.1 copy-start
Sparse Core Ops, SparseCore 0:
  128.4 120.2 reduce-scatter.1
  250.3 117.7 all-gather.1

commit v2 on v1

--- a/solution.py
+++ b/solution.py
@@ -72,13 +72,14 @@
 
 
 def spread_kernel(
-    out_ref, eg_ref, gw_ref, n_ref, eg_out,
-    nv, eg_v, route_s, route_r, x_s, x_r, y_s, y_r, d_s, d_r, eg_sem, local_sem, n_sem,
+    out_ref, eg_ref, w_ref, gw_ref, n_ref, eg_out, wg_ref,
+    nv, eg_v, wl, route_s, route_r, x_s, x_r, y_s, y_r, d_s, d_r, eg_sem, local_sem, n_sem, w_x, w_s, w_r,
 ):
     at = Place()
     senders, most, width = out_ref.shape
     half = eg_v.shape[2]
     rows = eg_v.shape[1]
+    groups = nv.shape[0]
     e, k, y, x, c = at.e, at.k, at.y, at.x, at.c
     ox = 1 - x
     c_y, c_k, c_ky = at.group(k, 1 - y), at.group(1 - k, y), at.group(1 - k, 1 - y)
@@ -117,6 +118,57 @@
     eg_in = send(eg_v.at[ox], eg_v.at[ox], eg_sem.at[0], eg_sem.at[1], at.x_peer)
 
     eg_load.start()
+    own_half = pl.ds(pl.multiple_of(x * half, LANES), half)
+    peer_half = pl.ds(pl.multiple_of(ox * half, LANES), half)
+    w_load = pltpu.make_async_copy(w_ref.at[:, own_half], wl, local_sem.at[1])
+    w_keep = pltpu.make_async_copy(wl, wg_ref.at[e], local_sem.at[2])
+    w_load.start()
+    z = e // 2
+    e_peer = e + 1 - 2 * x
+    w_swap = send(w_ref.at[:, peer_half], wg_ref.at[e], w_x.at[0], w_x.at[1], at.x_peer)
+    w_swap_in = send(wg_ref.at[e_peer], wg_ref.at[e_peer], w_x.at[0], w_x.at[1], at.x_peer)
+
+    def w_hop(b, src, way):
+        to = e + 2 if way == 0 else e - 2
+        return send(src, wg_ref.at[b], w_s.at[way, b], w_r.at[b], (to, k, y))
+
+    def room(way, distance):
+        if way == 0:
+            return (z >= distance) & (z + 1 < senders // 2)
+        return (z + distance < senders // 2) & (z >= 1)
+
+    def came(way, distance):
+        return z >= distance if way == 0 else z + distance < senders // 2
+
+    def block_from(way, distance, parity):
+        return 2 * (z - distance if way == 0 else z + distance) + parity
+
+    def w_own(b, src):
+        for way in range(2):
+            @pl.when(room(way, 0))
+            def _():
+                w_hop(b, src, way).start()
+
+    def w_relay(distance):
+        for parity in (x, ox):
+            for way in range(2):
+                @pl.when(came(way, distance))
+                def _():
+                    b = block_from(way, distance, parity)
+                    w_hop(b, wg_ref.at[b], way).wait_recv()
+
+                    @pl.when(room(way, distance))
+                    def _():
+                        w_hop(b, wg_ref.at[b], way).start()
+
+    def w_sent(distance):
+        for parity in (x, ox):
+            for way in range(2):
+                @pl.when(room(way, distance))
+                def _():
+                    b = block_from(way, distance, parity)
+                    w_hop(b, wg_ref.at[b], way).wait_send()
+
     at.greet()
 
     def over(fn, start=0):
@@ -127,6 +179,10 @@
     x_hop(e, own).start()
     y_hop(x, e, own).start()
     k_hop(y, x, e, own).start()
+    w_swap.start()
+    w_load.wait()
+    w_own(e, wl)
+    w_keep.start()
     nv[c, x, e] = out_ref[e]
 
     def pass_on(step):
@@ -139,6 +195,8 @@
 
     over(pass_on, 1)
     eg_send.start()
+    w_swap_in.wait_recv()
+    w_own(e_peer, wg_ref.at[e_peer])
 
     def pass_x(step):
         s = at.other(step)
@@ -148,6 +206,7 @@
         k_hop(y, ox, s, ref).start()
 
     over(pass_x)
+    w_relay(1)
 
     def product(group):
         total = None
@@ -185,6 +244,7 @@
     keep(1, c_k)
     product(c_k)
     pass_y(ox)
+    w_relay(2)
     keep(2, c_y)
     product(c_y)
 
@@ -196,6 +256,12 @@
     keep(3, c_ky)
     product(c_ky)
 
+    for distance in range(3, groups):
+        w_relay(distance)
+    for distance in range(groups):
+        w_sent(distance)
+    w_swap.wait_send()
+    w_keep.wait()
     over(lambda step: route(at.other(step)).wait_send(), 1)
 
     def sent(step):
@@ -213,7 +279,7 @@
         pltpu.make_async_copy(nv.at[group], n_ref.at[group], n_sem.at[i]).wait()
 
 
-def spread(outgoing, embed_grad):
+def spread(outgoing, embed_grad, proj_weight):
     senders, most, width = outgoing.shape
     groups = 4
     rows, cols = embed_grad.shape
@@ -227,15 +293,17 @@
             jax.ShapeDtypeStruct((groups * width, half), BF16),
             jax.ShapeDtypeStruct((groups, 2, senders, most, width), BF16),
             jax.ShapeDtypeStruct((2, rows, half), BF16),
-        ),
-        in_specs=[vmem, any_spec],
-        out_specs=(vmem, any_spec, any_spec),
+            jax.ShapeDtypeStruct((senders, proj_weight.shape[0], half), BF16),
+        ),
+        in_specs=[vmem, any_spec, any_spec],
+        out_specs=(vmem, any_spec, any_spec, any_spec),
         scratch_shapes=[
             pltpu.VMEM((groups, 2, senders, most, width), BF16),
             pltpu.VMEM((2, rows, half), BF16),
+            pltpu.VMEM((proj_weight.shape[0], half), BF16),
             dma((senders,)), dma((senders,)), dma((senders,)), dma((senders,)),
             dma((2, senders)), dma((2, senders)), dma((2, 2, senders)), dma((2, 2, senders)),
-            dma((2,)), dma((1,)), dma((groups,)),
+            dma((2,)), dma((3,)), dma((groups,)), dma((2,)), dma((2, senders)), dma((senders,)),
         ],
         compiler_params=pltpu.CompilerParams(
             collective_id=0, has_side_effects=True, vmem_limit_bytes=56 * 1024 * 1024
@@ -244,7 +312,7 @@
             flops=60 * 10**9, bytes_accessed=32 * rows * half, transcendentals=0
         ),
         name="spread",
-    )(outgoing, embed_grad)
+    )(outgoing, embed_grad, proj_weight)
 
 
 def finish_kernel(
@@ -268,11 +336,14 @@
         lax.fori_loop(0, senders, lambda i, carry: (fn(i), carry)[1], 0)
 
     def product(group):
-        for w in range(2):
+        def one(w, carry):
             total = lax.dot_general(
                 eg_ref[w], w_ref[group], (((1,), (1,)), ((), ())), preferred_element_type=F32
             )
             dv[group, w] = total.astype(BF16).reshape(senders, most, width)
+            return carry
+
+        lax.fori_loop(0, 2, one, 0)
 
     def core(v, s):
         return send(
@@ -409,6 +480,122 @@
     )(shared, weight, grads)
 
 
+def row_kernel(mine, total, seen, send_sem, recv_sem):
+    at = Place()
+    groups = seen.shape[0]
+    peers = [(k, y) for k in range(2) for y in range(2)]
+    barrier = pltpu.get_barrier_semaphore()
+
+    def others(fn):
+        for k, y in peers:
+            @pl.when(at.group(k, y) != at.c)
+            def _():
+                fn(k, y)
+
+    others(
+        lambda k, y: pl.semaphore_signal(barrier, inc=1, device_id=(at.e, k, y), device_id_type=MESH)
+    )
+    pl.semaphore_wait(barrier, groups - 1)
+
+    def copy(k, y, slot):
+        g = at.group(k, y)
+        return send(mine, seen.at[slot], send_sem.at[g], recv_sem.at[slot], (at.e, k, y))
+
+    others(lambda k, y: copy(k, y, at.c).start())
+    seen[at.c] = mine[...]
+    others(lambda k, y: copy(k, y, at.group(k, y)).wait_recv())
+    result = seen[0]
+    for g in range(1, groups):
+        result = result + seen[g]
+    total[...] = result
+    others(lambda k, y: copy(k, y, at.c).wait_send())
+
+
+def sum_rows(rows, groups):
+    vmem = pl.BlockSpec(memory_space=pltpu.VMEM)
+    return pl.pallas_call(
+        row_kernel,
+        out_shape=jax.ShapeDtypeStruct(rows.shape, F32),
+        in_specs=[vmem],
+        out_specs=vmem,
+        scratch_shapes=[
+            pltpu.VMEM((groups, *rows.shape), F32),
+            pltpu.SemaphoreType.DMA((groups,)),
+            pltpu.SemaphoreType.DMA((groups,)),
+        ],
+        compiler_params=pltpu.CompilerParams(collective_id=2, has_side_effects=True),
+        name="sum_rows",
+    )(rows)
+
+
+def both_kernel(mine, mine_cols, total, total_cols, seen, seen_cols, r_s, r_r, c_s, c_r):
+    at = Place()
+    groups, senders = seen.shape[0], seen_cols.shape[0]
+    peers = [(k, y) for k in range(2) for y in range(2)]
+    barrier = pltpu.get_barrier_semaphore()
+
+    def others(fn):
+        for k, y in peers:
+            @pl.when(at.group(k, y) != at.c)
+            def _():
+                fn(k, y)
+
+    def along(fn):
+        lax.fori_loop(1, senders, lambda i, carry: (fn(at.other(i)), carry)[1], 0)
+
+    def signal(device):
+        pl.semaphore_signal(barrier, inc=1, device_id=device, device_id_type=MESH)
+
+    others(lambda k, y: signal((at.e, k, y)))
+    along(lambda d: signal((d, at.k, at.y)))
+    pl.semaphore_wait(barrier, groups + senders - 2)
+
+    def copy(k, y, slot):
+        g = at.group(k, y)
+        return send(mine, seen.at[slot], r_s.at[g], r_r.at[slot], (at.e, k, y))
+
+    def col(d, slot):
+        return send(mine_cols, seen_cols.at[slot], c_s.at[d], c_r.at[slot], (d, at.k, at.y))
+
+    others(lambda k, y: copy(k, y, at.c).start())
+    along(lambda d: col(d, at.e).start())
+    seen[at.c] = mine[...]
+    seen_cols[at.e] = mine_cols[...]
+    others(lambda k, y: copy(k, y, at.group(k, y)).wait_recv())
+    along(lambda d: col(d, d).wait_recv())
+    result = seen[0]
+    for g in range(1, groups):
+        result = result + seen[g]
+    total[...] = result
+    result = seen_cols[0]
+    for d in range(1, senders):
+        result = result + seen_cols[d]
+    total_cols[...] = result
+    others(lambda k, y: copy(k, y, at.c).wait_send())
+    along(lambda d: col(d, at.e).wait_send())
+
+
+def sum_both(rows, cols, groups, senders):
+    vmem = pl.BlockSpec(memory_space=pltpu.VMEM)
+    dma = pltpu.SemaphoreType.DMA
+    return pl.pallas_call(
+        both_kernel,
+        out_shape=(
+            jax.ShapeDtypeStruct(rows.shape, F32),
+            jax.ShapeDtypeStruct(cols.shape, F32),
+        ),
+        in_specs=[vmem, vmem],
+        out_specs=(vmem, vmem),
+        scratch_shapes=[
+            pltpu.VMEM((groups, *rows.shape), F32),
+            pltpu.VMEM((senders, *cols.shape), F32),
+            dma((groups,)), dma((groups,)), dma((senders,)), dma((senders,)),
+        ],
+        compiler_params=pltpu.CompilerParams(collective_id=3, has_side_effects=True),
+        name="sum_both",
+    )(rows, cols)
+
+
 def owner_body(patches, gain, shift, proj_weight, llm_rank, embed_grad):
     features = ("section", "llmdp")
     own_rows, owned_width = patches.shape
@@ -422,14 +609,12 @@
     def near_exchange(v, split, concat):
         return lax.all_to_all(v, "enc", split, concat, axis_index_groups=near, tiled=True)
 
-    weight_part = near_exchange(proj_weight, 1, 0)
-    weight = lax.all_gather(weight_part, "enc", axis=0, axis_index_groups=far, tiled=True)
-
+    groups = width // owned_width
     column_start = lax.axis_index(features) * owned_width
     gain_own = lax.dynamic_slice_in_dim(gain, column_start, owned_width, 0)
     shift_own = lax.dynamic_slice_in_dim(shift, column_start, owned_width, 0)
     values = patches.astype(F32)
-    total, squares = lax.psum((jnp.sum(values, 1), jnp.sum(values * values, 1)), features)
+    total, squares = sum_rows(jnp.stack([jnp.sum(values, 1), jnp.sum(values * values, 1)]), groups)
     average = (total / width)[:, None]
     variance = (squares / width)[:, None] - average * average
     deviation = lax.rsqrt(variance + EPSILON)
@@ -440,8 +625,8 @@
     places = jnp.arange(senders * most_slots, dtype=jnp.int32)
     chosen = (places[:, None] == slot[None, :]).astype(BF16)
     outgoing = jnp.dot(chosen, normed, preferred_element_type=F32).astype(BF16)
-    grad_partial, shared, grads = spread(
-        outgoing.reshape(senders, most_slots, owned_width), embed_grad
+    grad_partial, shared, grads, weight = spread(
+        outgoing.reshape(senders, most_slots, owned_width), embed_grad, proj_weight
     )
     grad_part = lax.psum_scatter(
         grad_partial, "enc", scatter_dimension=0, axis_index_groups=far, tiled=True
@@ -449,23 +634,23 @@
     grad_weight = near_exchange(grad_part, 0, 1).astype(F32)
 
     embeds_recv, returned = finish(
-        shared, weight.reshape(width // owned_width, owned_width, weight.shape[1]), grads
+        shared, weight.reshape(groups, owned_width, weight.shape[2]), grads
     )
     dnormed = lax.dot_general(
         chosen, returned.reshape(senders * most_slots, owned_width), (((0,), (0,)), ((), ())),
         preferred_element_type=F32,
     )
     dxhat = dnormed * gain_own
-    mean_sum, cross_sum = lax.psum(
-        (jnp.sum(dxhat, 1), jnp.sum(dxhat * standardized, 1)), features
+    (mean_sum, cross_sum), (gain_gradient, grad_shift) = sum_both(
+        jnp.stack([jnp.sum(dxhat, 1), jnp.sum(dxhat * standardized, 1)]),
+        jnp.stack([jnp.sum(dnormed * standardized, 0), jnp.sum(dnormed, 0)]),
+        groups,
+        senders,
     )
     hidden_state_gradient = (
         deviation
         * (dxhat - (mean_sum / width)[:, None] - standardized * (cross_sum / width)[:, None])
     ).astype(BF16)
-    gain_gradient, grad_shift = lax.psum(
-        (jnp.sum(dnormed * standardized, 0), jnp.sum(dnormed, 0)), "enc"
-    )
     return (embeds_recv, hidden_state_gradient, grad_weight, gain_gradient, grad_shift)
 
 

time: 557 us -> 360 us (0.65); the launches traced: 549 us -> 359 us
  waiting for transfers between devices: 211 us -> 0.04 us
  Pallas kernels: 243 us -> 318 us
  blocking collectives: 59 us -> 0 us
    all_gather x1 -> x0, waiting for transfers between devices: 116 us -> none  [owner_body(): lax.all_gather(weight_part, 'enc', axis=0, axis_index_groups=far, tiled=T...]
    reduce_scatter x1, waiting for transfers between devices: 95 us -> 0.02 us  [owner_body(): lax.psum_scatter(grad_partial, 'enc', scatter_dimension=0, axis_index_gro...]
    pallas_call x1, Pallas kernels: 105 us -> 147 us  [spread(): pl.pallas_call(spread_kernel, out_shape=(jax.ShapeDtypeStruct((groups * w...]
    psum x3 -> x0, blocking collectives: 35.1 us -> none  [the longest x1 20.9 us: owner_body(): lax.psum((jnp.sum(dnormed * standardized, 0), jnp.sum(dnormed, 0)), 'enc')]
    pallas_call x0 -> x2, Pallas kernels: none -> 25.9 us  [the longest x1 21 us: sum_both(): pl.pallas_call(both_kernel, out_shape=(jax.ShapeDtypeStruct(rows.shape, F...]
    all_to_all x1 -> x0, blocking collectives: 23.9 us -> none  [near_exchange(): lax.all_to_all(v, 'enc', split, concat, axis_index_groups=near, tiled=True)]
    pallas_call x1, Pallas kernels: 138 us -> 145 us  [finish(): pl.pallas_call(finish_kernel, out_shape=(jax.ShapeDtypeStruct((rows, 2 *...]
  transfers between devices with their start and end apart: 3 -> 2, of which waited for: 2 -> 0; matrix products, arithmetic and copies ran while one was open for 1% -> 2% of each run, Pallas kernels for 25% -> 46%
where the time goes in v2:
time: 360 us; the launch traced here: 359 us
  Pallas kernels  318 us (88%)
  between operations  14.1 us (4%)
  local copies, waits for them, and re-layouts  9.45 us (3%)
  other arithmetic  8.55 us (2%)
  starting transfers between devices  5.24 us (1%)
  matrix products  3.96 us (1%)
    pallas_call x1, Pallas kernels, spread(): pl.pallas_call(spread_kernel, out_shape=(jax.ShapeDtypeStruct((groups * w...  147 us
    pallas_call x1, Pallas kernels, finish(): pl.pallas_call(finish_kernel, out_shape=(jax.ShapeDtypeStruct((rows, 2 *...  145 us
    pallas_call x1, Pallas kernels, sum_both(): pl.pallas_call(both_kernel, out_shape=(jax.ShapeDtypeStruct(rows.shape, F...  21 us
  transfers between devices with their start and end apart: 2, of which 0 were waited for; matrix products, arithmetic and copies ran while one was open for 2% of the time, Pallas kernels for 46%

profile of v2, /device:TPU:28, one launch (start us, length us, event | category | flops | bytes accessed | tf_op | source)
XLA Modules:
  0.0 359.4 jit_solution(15815256004476955281)
XLA Ops:
  7.2 1.2 convert_reduce_fusion
  8.4 0.6 pad_maximum_fusion.1.mine
  9.0 4.9 %sum_rows.1 = f32[2,256]{1,0:T(2,128)} custom-call(f32[2,256]{1,0:T(2,128)} %pad_maximum_fusion.1.mine), custom_call_target="tpu_custom_call" | custom-call | tf_op jit(solution)/shard_map/sum_rows/pallas_call | solution.py:516
  13.9 0.8 slice_multiply_fusion.3
  14.7 0.8 dynamic_slice.6
  15.4 0.8 dynamic_slice.7
  16.2 0.7 fusion.23
  17.7 0.8 fusion.22
  18.5 0.7 multiply_add_fusion
  19.2 1.6 convolution_convert_fusion
  20.8 1.6 copy.13
  22.4 146.9 %spread.1 = (bf16[3200,1024]{1,0:T(8,128)(2,1)}, bf16[4,2,8,96,800]{4,3,2,1,0:T(8,128)(2,1)}, bf16[2,768,1024]{2,1,0:T(8,128)(2,1)}, bf16[8,400,1024]{2,1,0:T(8,128)(2,1)}) custom-call(bf16[8,96,800]{2,1,0:T(8,128)(2,1)} %bitcast.29, bf16[768,2048]{1,0:T(8,128)(2,1)} %eg_ref.1, bf16[400,2048]{1,0:T(8,128)(2,1)} %w_ref.1), custom_call_target="tpu_custom_call" | custom-call | flops 60000002048 | bytes 25165824 | tf_op jit(solution)/shard_map/spread/pallas_call | solution.py:290
  169.3 145.3 %finish.1 = (bf16[768,2048]{1,0:T(8,128)(2,1)}, bf16[8,96,800]{2,1,0:T(8,128)(2,1)}) custom-call(bf16[4,2,8,96,800]{4,3,2,1,0:T(8,128)(2,1)} %get-tuple-element.13.n_ref, bf16[4,800,1024]{2,1,0:T(8,128)(2,1)} %bitcast.44, bf16[2,768,1024]{2,1,0:T(8,128)(2,1)} %get-tuple-element.15.eg_ref), custom_call_target="tpu_custom_call" | custom-call | flops 60000002048 | bytes 25165824 | tf_op jit(solution)/shard_map/finish/pallas_call | solution.py:453
  314.6 2.3 fusion.9
  317.0 5.2 %all-to-all-start = ((bf16[2,400,1024]{2,1,0:T(8,128)(2,1)}), bf16[2,400,1024]{2,1,0:T(8,128)(2,1)S(1)}, u32[]{:S(2)}, u32[]{:S(2)}) async-start(bf16[2,400,1024]{2,1,0:T(8,128)(2,1)} %bitcast.28), calls=%async_computation.1 | async-start | bytes 3276800 | tf_op jit(solution)/shard_map/all_to_all | solution.py:610
  322.2 0.6 pad_maximum_fusion.2.mine
  322.7 0.6 pad_maximum_fusion.mine_cols
  323.4 21.0 %sum_both.1 = (f32[2,256]{1,0:T(2,128)}, f32[2,800]{1,0:T(2,128)}) custom-call(f32[2,256]{1,0:T(2,128)} %pad_maximum_fusion.2.mine, f32[2,800]{1,0:T(2,128)} %pad_maximum_fusion.mine_cols), custom_call_target="tpu_custom_call" | custom-call | tf_op jit(solution)/shard_map/sum_both/pallas_call | solution.py:581
  344.3 1.4 slice_reduce_fusion.1
  345.7 0.7 slice_multiply_fusion.1
  346.5 1.0 fusion.12
  347.9 1.9 copy.15
  349.8 1.1 copy-done
  350.9 1.7 copy.17
  (15 shorter events, 1.3 us)
Async XLA Ops:
  7.2 309.8 %reduce-scatter.2.cloned.1.call-start = ((), (), s32[]{:S(2)}) async-start(), calls=%async_computation.2 | async-start | bytes 8192000 | tf_op jit(solution)/shard_map/reduce_scatter | solution.py:631
  169.3 145.3 %copy-start.1 = (bf16[256,800]{0,1:T(8,128)(2,1)S(1)}, bf16[256,800]{0,1:T(8,128)(2,1)}, u32[]{:S(2)}) copy-start(bf16[256,800]{0,1:T(8,128)(2,1)} %param.6) | copy-start | bytes 1228804
  317.0 30.5 %all-to-all-start = ((bf16[2,400,1024]{2,1,0:T(8,128)(2,1)}), bf16[2,400,1024]{2,1,0:T(8,128)(2,1)S(1)}, u32[]{:S(2)}, u32[]{:S(2)}) async-start(bf16[2,400,1024]{2,1,0:T(8,128)(2,1)} %bitcast.28), calls=%async_computation.1 | async-start | bytes 3276800 | tf_op jit(solution)/shard_map/all_to_all | solution.py:610
  347.9 3.1 copy-start
Sparse Core Ops, SparseCore 0:
  169.4 136.5 reduce-scatter.1

commit v3 on v2

--- a/solution.py
+++ b/solution.py
@@ -71,142 +71,179 @@
     )
 
 
+def loop(count, fn, start=0):
+    lax.fori_loop(start, count, lambda i, carry: (fn(i), carry)[1], 0)
+
+
+class Line:
+    def __init__(self, at):
+        self.z = at.e // 2
+        self.count = at.senders // 2
+        self.parities = (at.x, 1 - at.x)
+
+    def came(self, way, distance):
+        return self.z >= distance if way == 0 else self.z + distance < self.count
+
+    def room(self, way, distance):
+        if way == 0:
+            return (self.z >= distance) & (self.z + 1 < self.count)
+        return (self.z + distance < self.count) & (self.z >= 1)
+
+    def block(self, way, distance, parity):
+        return 2 * (self.z - distance if way == 0 else self.z + distance) + parity
+
+    def visit(self, distance, condition, fn):
+        for parity in self.parities:
+            for way in range(2):
+                @pl.when(condition(way, distance))
+                def _():
+                    fn(way, self.block(way, distance, parity))
+
+
 def spread_kernel(
     out_ref, eg_ref, w_ref, gw_ref, n_ref, eg_out, wg_ref,
-    nv, eg_v, wl, route_s, route_r, x_s, x_r, y_s, y_r, d_s, d_r, eg_sem, local_sem, n_sem, w_x, w_s, w_r,
+    nv, eg_v, wl, route_s, route_r, x_s, x_r, y_s, y_r, d_s, d_r, eg_s, eg_r, local_sem, n_sem, w_x, w_s, w_r,
 ):
     at = Place()
+    line = Line(at)
     senders, most, width = out_ref.shape
-    half = eg_v.shape[2]
-    rows = eg_v.shape[1]
+    rows, half = eg_v.shape[1:]
     groups = nv.shape[0]
-    e, k, y, x, c = at.e, at.k, at.y, at.x, at.c
+    chips = senders // 2
+    e, k, y, x, c, z = at.e, at.k, at.y, at.x, at.c, line.z
     ox = 1 - x
+    e_peer = e + 1 - 2 * x
     c_y, c_k, c_ky = at.group(k, 1 - y), at.group(1 - k, y), at.group(1 - k, 1 - y)
-
-    def route(d):
-        return send(out_ref.at[d], nv.at[c, lax.rem(d, 2), e], route_s.at[d], route_r.at[e], (d, k, y))
-
-    def route_in(s):
-        return send(out_ref.at[s], nv.at[c, x, s], route_s.at[s], route_r.at[s], (s, k, y))
-
-    def x_hop(s, src):
-        return send(src, nv.at[c, x, s], x_s.at[s], x_r.at[s], at.x_peer)
-
-    def x_in(s):
-        return send(nv.at[c, ox, s], nv.at[c, ox, s], x_s.at[s], x_r.at[s], at.x_peer)
-
-    def y_hop(w, s, src):
-        return send(src, nv.at[c, w, s], y_s.at[w, s], y_r.at[w, s], at.y_peer)
-
-    def y_in(w, s):
-        return send(nv.at[c_y, w, s], nv.at[c_y, w, s], y_s.at[w, s], y_r.at[w, s], at.y_peer)
-
-    def k_hop(v, w, s, src):
-        return send(src, nv.at[at.group(k, v), w, s], d_s.at[v, w, s], d_r.at[v, w, s], at.k_peer)
-
-    def k_in(v, w, s):
-        ref = nv.at[at.group(1 - k, v), w, s]
-        return send(ref, ref, d_s.at[v, w, s], d_r.at[v, w, s], at.k_peer)
-
-    eg_send = send(
-        eg_ref.at[:, pl.ds(pl.multiple_of(ox * half, LANES), half)], eg_v.at[x], eg_sem.at[0], eg_sem.at[1], at.x_peer
-    )
-    eg_load = pltpu.make_async_copy(
-        eg_ref.at[:, pl.ds(pl.multiple_of(x * half, LANES), half)], eg_v.at[x], local_sem.at[0]
-    )
-    eg_in = send(eg_v.at[ox], eg_v.at[ox], eg_sem.at[0], eg_sem.at[1], at.x_peer)
-
-    eg_load.start()
     own_half = pl.ds(pl.multiple_of(x * half, LANES), half)
     peer_half = pl.ds(pl.multiple_of(ox * half, LANES), half)
+
+    def chip(i):
+        return lax.rem(z + i, chips)
+
+    def route(to, w):
+        return send(
+            out_ref.at[2 * to + w], nv.at[c, w, e], route_s.at[to, w], route_r.at[z, w], (2 * to + x, k, y)
+        )
+
+    def route_in(s, w):
+        ref = nv.at[c, w, 2 * s + x]
+        return send(ref, ref, route_s.at[s, w], route_r.at[s, w], (2 * s + x, k, y))
+
+    def x_hop(s, w, src):
+        return send(src, nv.at[c, w, 2 * s + x], x_s.at[s, w], x_r.at[s, w], at.x_peer)
+
+    def x_in(s, w):
+        ref = nv.at[c, w, 2 * s + ox]
+        return send(ref, ref, x_s.at[s, w], x_r.at[s, w], at.x_peer)
+
+    def y_hop(s, w, src):
+        return send(src, nv.at[c, w, s], y_s.at[s, w], y_r.at[s, w], at.y_peer)
+
+    def y_in(s, w):
+        ref = nv.at[c_y, w, s]
+        return send(ref, ref, y_s.at[s, w], y_r.at[s, w], at.y_peer)
+
+    def k_hop(v, s, w, src):
+        return send(src, nv.at[at.group(k, v), w, s], d_s.at[v, s, w], d_r.at[v, s, w], at.k_peer)
+
+    def k_in(v, s, w):
+        ref = nv.at[at.group(1 - k, v), w, s]
+        return send(ref, ref, d_s.at[v, s, w], d_r.at[v, s, w], at.k_peer)
+
+    def eg_piece(i):
+        part = pl.ds(pl.multiple_of(i * most, SUBLANES), most)
+        return send(eg_ref.at[part, peer_half], eg_v.at[x, part], eg_s.at[i], eg_r.at[i], at.x_peer)
+
+    def eg_in(i):
+        ref = eg_v.at[ox, pl.ds(pl.multiple_of(i * most, SUBLANES), most)]
+        return send(ref, ref, eg_s.at[i], eg_r.at[i], at.x_peer)
+
+    eg_load = pltpu.make_async_copy(eg_ref.at[:, own_half], eg_v.at[x], local_sem.at[0])
     w_load = pltpu.make_async_copy(w_ref.at[:, own_half], wl, local_sem.at[1])
     w_keep = pltpu.make_async_copy(wl, wg_ref.at[e], local_sem.at[2])
-    w_load.start()
-    z = e // 2
-    e_peer = e + 1 - 2 * x
     w_swap = send(w_ref.at[:, peer_half], wg_ref.at[e], w_x.at[0], w_x.at[1], at.x_peer)
     w_swap_in = send(wg_ref.at[e_peer], wg_ref.at[e_peer], w_x.at[0], w_x.at[1], at.x_peer)
 
-    def w_hop(b, src, way):
+    def w_hop(way, b, src=None):
         to = e + 2 if way == 0 else e - 2
-        return send(src, wg_ref.at[b], w_s.at[way, b], w_r.at[b], (to, k, y))
-
-    def room(way, distance):
-        if way == 0:
-            return (z >= distance) & (z + 1 < senders // 2)
-        return (z + distance < senders // 2) & (z >= 1)
-
-    def came(way, distance):
-        return z >= distance if way == 0 else z + distance < senders // 2
-
-    def block_from(way, distance, parity):
-        return 2 * (z - distance if way == 0 else z + distance) + parity
+        return send(
+            wg_ref.at[b] if src is None else src, wg_ref.at[b], w_s.at[way, b], w_r.at[b],
+            (2 * (to // 2) + x, k, y),
+        )
 
     def w_own(b, src):
         for way in range(2):
-            @pl.when(room(way, 0))
+            @pl.when(line.room(way, 0))
             def _():
-                w_hop(b, src, way).start()
-
-    def w_relay(distance):
-        for parity in (x, ox):
-            for way in range(2):
-                @pl.when(came(way, distance))
+                w_hop(way, b, src).start()
+
+    def w_relay(distance, last):
+        def one(way, b):
+            w_hop(way, b).wait_recv()
+            if not last:
+                @pl.when(line.room(way, distance))
                 def _():
-                    b = block_from(way, distance, parity)
-                    w_hop(b, wg_ref.at[b], way).wait_recv()
-
-                    @pl.when(room(way, distance))
-                    def _():
-                        w_hop(b, wg_ref.at[b], way).start()
-
-    def w_sent(distance):
-        for parity in (x, ox):
-            for way in range(2):
-                @pl.when(room(way, distance))
-                def _():
-                    b = block_from(way, distance, parity)
-                    w_hop(b, wg_ref.at[b], way).wait_send()
-
+                    w_hop(way, b).start()
+
+        line.visit(distance, line.came, one)
+
+    eg_load.start()
+    w_load.start()
     at.greet()
-
-    def over(fn, start=0):
-        lax.fori_loop(start, senders, lambda i, carry: (fn(i), carry)[1], 0)
-
-    over(lambda step: route(at.other(step)).start(), 1)
-    own = out_ref.at[e]
-    x_hop(e, own).start()
-    y_hop(x, e, own).start()
-    k_hop(y, x, e, own).start()
+    for w in range(2):
+        loop(chips, lambda i: route(chip(i), w).start(), 1)
     w_swap.start()
     w_load.wait()
     w_own(e, wl)
     w_keep.start()
-    nv[c, x, e] = out_ref[e]
-
-    def pass_on(step):
-        s = at.other(step)
-        ref = nv.at[c, x, s]
-        route_in(s).wait_recv()
-        x_hop(s, ref).start()
-        y_hop(x, s, ref).start()
-        k_hop(y, x, s, ref).start()
-
-    over(pass_on, 1)
-    eg_send.start()
+
+    def pass_on(s, w, src):
+        x_hop(s, w, src).start()
+        y_hop(2 * s + x, w, src).start()
+        k_hop(y, 2 * s + x, w, src).start()
+
+    for w in range(2):
+        pass_on(z, w, out_ref.at[2 * z + w])
+        eg_piece(w).start()
+        nv[c, w, e] = out_ref[2 * z + w]
+
+    def pass_route(i):
+        s = chip(i)
+        for w in range(2):
+            route_in(s, w).wait_recv()
+            pass_on(s, w, nv.at[c, w, 2 * s + x])
+            eg_piece(2 * i + w).start()
+
+    loop(chips, pass_route, 1)
     w_swap_in.wait_recv()
     w_own(e_peer, wg_ref.at[e_peer])
 
-    def pass_x(step):
-        s = at.other(step)
-        ref = nv.at[c, ox, s]
-        x_in(s).wait_recv()
-        y_hop(ox, s, ref).start()
-        k_hop(y, ox, s, ref).start()
-
-    over(pass_x)
-    w_relay(1)
+    def pass_x(i):
+        s = chip(i)
+        for w in range(2):
+            x_in(s, w).wait_recv()
+            ref = nv.at[c, w, 2 * s + ox]
+            y_hop(2 * s + ox, w, ref).start()
+            k_hop(y, 2 * s + ox, w, ref).start()
+
+    loop(chips, pass_x)
+    w_relay(1, groups == 3)
+
+    def pass_y(parity):
+        def one(i):
+            s = 2 * chip(i) + parity
+            for w in range(2):
+                y_in(s, w).wait_recv()
+                k_hop(1 - y, s, w, nv.at[c_y, w, s]).start()
+
+        loop(chips, one)
+
+    def wait_core(v):
+        def one(s):
+            for w in range(2):
+                k_in(v, s, w).wait_recv()
+
+        loop(senders, one)
 
     def product(group):
         total = None
@@ -220,60 +257,42 @@
     def keep(i, group):
         pltpu.make_async_copy(nv.at[group], n_ref.at[group], n_sem.at[i]).start()
 
-    def pass_y(w):
-        def one(step):
-            s = at.other(step)
-            y_in(w, s).wait_recv()
-            k_hop(1 - y, w, s, nv.at[c_y, w, s]).start()
-
-        over(one)
-
-    keep(0, c)
+    pass_y(x)
     eg_load.wait()
-    eg_in.wait_recv()
+    loop(senders, lambda i: eg_in(i).wait_recv())
     eg_keep = pltpu.make_async_copy(eg_v, eg_out, local_sem.at[0])
     eg_keep.start()
+    keep(0, c)
     product(c)
-    pass_y(x)
-
-    def near_in(step):
-        for w in range(2):
-            k_in(y, w, at.other(step)).wait_recv()
-
-    over(near_in)
+    wait_core(y)
     keep(1, c_k)
     product(c_k)
     pass_y(ox)
-    w_relay(2)
     keep(2, c_y)
     product(c_y)
-
-    def far_in(step):
-        for w in range(2):
-            k_in(1 - y, w, at.other(step)).wait_recv()
-
-    over(far_in)
+    wait_core(1 - y)
     keep(3, c_ky)
     product(c_ky)
-
-    for distance in range(3, groups):
-        w_relay(distance)
-    for distance in range(groups):
-        w_sent(distance)
+    for distance in range(2, groups - 1):
+        w_relay(distance, distance == groups - 2)
+
+    for distance in range(groups - 2):
+        line.visit(distance, line.room, lambda way, b: w_hop(way, b).wait_send())
     w_swap.wait_send()
     w_keep.wait()
-    over(lambda step: route(at.other(step)).wait_send(), 1)
-
-    def sent(step):
-        s = at.other(step)
-        x_hop(s, nv.at[c, x, s]).wait_send()
+    for w in range(2):
+        loop(chips, lambda i: route(chip(i), w).wait_send(), 1)
+
+    def sent(s):
+        eg_piece(s).wait_send()
         for w in range(2):
-            y_hop(w, s, nv.at[c, w, s]).wait_send()
+            y_hop(s, w, nv.at[c, w, s]).wait_send()
             for v in range(2):
-                k_hop(v, w, s, nv.at[at.group(k, v), w, s]).wait_send()
-
-    over(sent)
-    eg_send.wait_send()
+                k_hop(v, s, w, nv.at[at.group(k, v), w, s]).wait_send()
+
+    loop(senders, sent)
+    for w in range(2):
+        loop(chips, lambda s: x_hop(s, w, nv.at[c, w, 2 * s + x]).wait_send())
     eg_keep.wait()
     for i, group in enumerate((c, c_k, c_y, c_ky)):
         pltpu.make_async_copy(nv.at[group], n_ref.at[group], n_sem.at[i]).wait()
@@ -281,7 +300,8 @@
 
 def spread(outgoing, embed_grad, proj_weight):
     senders, most, width = outgoing.shape
-    groups = 4
+    chips = senders // 2
+    groups = chips
     rows, cols = embed_grad.shape
     half = cols // 2
     dma = pltpu.SemaphoreType.DMA
@@ -301,9 +321,9 @@
             pltpu.VMEM((groups, 2, senders, most, width), BF16),
             pltpu.VMEM((2, rows, half), BF16),
             pltpu.VMEM((proj_weight.shape[0], half), BF16),
-            dma((senders,)), dma((senders,)), dma((senders,)), dma((senders,)),
-            dma((2, senders)), dma((2, senders)), dma((2, 2, senders)), dma((2, 2, senders)),
-            dma((2,)), dma((3,)), dma((groups,)), dma((2,)), dma((2, senders)), dma((senders,)),
+            dma((chips, 2)), dma((chips, 2)), dma((chips, 2)), dma((chips, 2)),
+            dma((senders, 2)), dma((senders, 2)), dma((2, senders, 2)), dma((2, senders, 2)),
+            dma((senders,)), dma((senders,)), dma((3,)), dma((groups,)), dma((2,)), dma((2, senders)), dma((senders,)),
         ],
         compiler_params=pltpu.CompilerParams(
             collective_id=0, has_side_effects=True, vmem_limit_bytes=56 * 1024 * 1024
@@ -316,29 +336,160 @@
 
 
 def finish_kernel(
-    n_ref, w_ref, eg_ref, emb_ref, t_ref,
-    nv, dv, ra, yb, xb, rb, ev, a_s, a_r, b_s, b_r, c_s, c_r, t_s, t_r, e_sem, n_sem, l_sem,
+    n_ref, wg_ref, eg_ref, g_ref, emb_ref, t_ref, sum_ref,
+    rv, gs, g_load, r_s, r_r, q_s, q_keep,
+    nv, wv, dv, ra, yb, xb, rb, ev, a_s, a_r, b_s, b_r, c_s, c_r, t_s, t_r, e_s, e_r, n_sem, l_sem, w_s, w_r, w_l,
 ):
     at = Place()
+    line = Line(at)
     senders, most, width = t_ref.shape
     rows, half = eg_ref.shape[1:]
-    e, k, y, x, c = at.e, at.k, at.y, at.x, at.c
+    groups = dv.shape[0]
+    e, k, y, x, c, z = at.e, at.k, at.y, at.x, at.c, line.z
     ox, oy, ok = 1 - x, 1 - y, 1 - k
     c_y = at.group(k, oy)
+    own_half = pl.ds(pl.multiple_of(x * half, LANES), half)
+    peer_half = pl.ds(pl.multiple_of(ox * half, LANES), half)
+
+    def turn(i):
+        return lax.select(z < groups // 2, i, groups - 1 - i)
+
+    last = turn(groups - 1)
+    distant = (last - z == groups - 1) | (z - last == groups - 1)
 
     def load(w):
         return pltpu.make_async_copy(n_ref.at[:, w], nv, n_sem.at[0])
 
+    def w_load(i):
+        pair = pl.ds(2 * turn(i), 2)
+        return pltpu.make_async_copy(wg_ref.at[pair], wv.at[pair], w_l.at[i])
+
+    def w_hop(way, b):
+        to = e + 2 if way == 0 else e - 2
+        return send(wg_ref.at[b], wv.at[b], w_s.at[way, b], w_r.at[b], (2 * (to // 2) + x, k, y))
+
+    for i in range(groups - 1):
+        w_load(i).start()
+
+    @pl.when(jnp.logical_not(distant))
+    def _():
+        w_load(groups - 1).start()
+
     load(ox).start()
     at.greet()
-
-    def over(fn):
-        lax.fori_loop(0, senders, lambda i, carry: (fn(i), carry)[1], 0)
+    line.visit(groups - 2, line.room, lambda way, b: w_hop(way, b).start())
+
+    chips = g_ref.shape[0]
+    piece_rows = g_ref.shape[2]
+    tile = piece_rows // 5
+    tiles = [pl.ds(i * tile, tile) for i in range(5)]
+
+    def g_get(way, d, j):
+        return pltpu.make_async_copy(g_ref.at[d, j], gs.at[way, j], g_load.at[way, j])
+
+    def sum_hop(way, d, j, src):
+        if way == 0:
+            to, slot = e + 2, d
+        else:
+            to, slot = e - 2, lax.select(d == z - 1, chips, d)
+        return send(
+            src, rv.at[slot, j], r_s.at[way, d, j], r_r.at[way, d, j], (2 * (to // 2) + x, k, y)
+        )
+
+    def sum_in(way, d, j):
+        return sum_hop(way, d, j, rv.at[d, j])
+
+    def upstream(way):
+        return z > 0 if way == 0 else z < chips - 1
+
+    def downstream(way, d):
+        return d > z if way == 0 else d < z
+
+    def goal(way, i):
+        return chips - 1 - i if way == 0 else i
+
+    def over_j(fn):
+        fn(ox)
+        fn(x)
+
+    for way in range(2):
+        @pl.when(jnp.logical_not(upstream(way)))
+        def _():
+            for i in range(chips - 1):
+                d = goal(way, i)
+                over_j(lambda j: sum_hop(way, d, j, g_ref.at[d, j]).start())
+
+    def relay(i, near):
+        for way in range(2):
+            d = goal(way, i)
+            mine = (z < chips // 2) if (way == 0) == near else (z >= chips // 2)
+
+            @pl.when(mine & upstream(way) & downstream(way, d))
+            def _():
+                over_j(lambda j: g_get(way, d, j).start())
+
+                def one(j):
+                    g_get(way, d, j).wait()
+                    sum_in(way, d, j).wait_recv()
+                    for t in tiles:
+                        rv[d, j, t] = (rv[d, j, t].astype(F32) + gs[way, j, t].astype(F32)).astype(BF16)
+                    sum_hop(way, d, j, rv.at[d, j]).start()
+
+                over_j(one)
+
+    def settle():
+        def one(j):
+            g_get(0, z, j).wait()
+            for way in range(2):
+                @pl.when(upstream(way))
+                def _():
+                    sum_in(way, z, j).wait_recv()
+
+            def close(*slots):
+                for t in tiles:
+                    total = gs[0, j, t].astype(F32)
+                    for slot in slots:
+                        total = total + rv[slot, j, t].astype(F32)
+                    rv[z, j, t] = total.astype(BF16)
+
+            @pl.when(z == 0)
+            def _():
+                close(chips)
+
+            @pl.when(z == chips - 1)
+            def _():
+                close(z)
+
+            @pl.when((z > 0) & (z < chips - 1))
+            def _():
+                close(z, chips)
+
+        over_j(lambda j: g_get(0, z, j).start())
+        one(ox)
+        swap.start()
+        one(x)
+        swap_keep.start()
+
+    swap = send(rv.at[z, ox], sum_ref.at[:, own_half], q_s.at[0], q_s.at[1], at.x_peer)
+    swap_in = send(sum_ref.at[:, peer_half], sum_ref.at[:, peer_half], q_s.at[0], q_s.at[1], at.x_peer)
+    swap_keep = pltpu.make_async_copy(rv.at[z, x], sum_ref.at[:, own_half], q_keep.at[0])
+
+    def sums_sent():
+        for way in range(2):
+            for i in range(chips - 1):
+                d = goal(way, i)
+
+                @pl.when(downstream(way, d))
+                def _():
+                    over_j(lambda j: sum_hop(way, d, j, rv.at[d, j]).wait_send())
+
+    def weights(group):
+        return wv[pl.ds(2 * group, 2)].reshape(width, half)
 
     def product(group):
         def one(w, carry):
             total = lax.dot_general(
-                eg_ref[w], w_ref[group], (((1,), (1,)), ((), ())), preferred_element_type=F32
+                eg_ref[w], weights(group), (((1,), (1,)), ((), ())), preferred_element_type=F32
             )
             dv[group, w] = total.astype(BF16).reshape(senders, most, width)
             return carry
@@ -350,10 +501,6 @@
             dv.at[at.group(ok, v), :, s], ra.at[v, :, s], a_s.at[v, s], a_r.at[v, s], at.k_peer
         )
 
-    product(at.group(ok, oy))
-    over(lambda s: core(oy, s).start())
-    product(c_y)
-
     def across(s):
         return send(dv.at[c_y, :, s], yb.at[:, s], b_s.at[s], b_r.at[s], at.y_peer)
 
@@ -362,25 +509,60 @@
         dv[c_y, :, s] = (dv[c_y, :, s].astype(F32) + ra[oy, :, s].astype(F32)).astype(BF16)
         across(s).start()
 
-    over(fold_core)
-    product(at.group(ok, y))
-    over(lambda s: core(y, s).start())
-    product(c)
+    def round_of(i):
+        group = turn(i)
+        product(group)
+
+        @pl.when(group // 2 != k)
+        def _():
+            loop(senders, lambda s: core(group - 2 * (group // 2), s).start())
+
+    def early(i):
+        w_load(i).wait()
+        round_of(i)
+
+    for i in range(groups - 1):
+        early(i)
+
+    @pl.when(last != c_y)
+    def _():
+        loop(senders, fold_core)
+
+    relay(0, True)
+
+    @pl.when(jnp.logical_not(distant))
+    def _():
+        w_load(groups - 1).wait()
+
+    line.visit(groups - 1, line.came, lambda way, b: w_hop(way, b).wait_recv())
+    round_of(groups - 1)
+
+    @pl.when(last == c_y)
+    def _():
+        loop(senders, fold_core)
 
     def embed(w):
         total = None
-        for group in range(w_ref.shape[0]):
+        for group in range(groups):
             term = jnp.dot(
-                nv[group].reshape(rows, width), w_ref[group], preferred_element_type=F32
+                nv[group].reshape(rows, width), weights(group), preferred_element_type=F32
             )
             total = term if total is None else total + term
-        return total.astype(BF16)
-
-    own_cols = pl.ds(pl.multiple_of(x * half, LANES), half)
+        ev[w] = total.astype(BF16)
+
+    def part(s):
+        return pl.ds(pl.multiple_of(s * most, SUBLANES), most)
+
+    def emb_piece(s):
+        return send(ev.at[ox, part(s)], emb_ref.at[part(s), own_half], e_s.at[s], e_r.at[s], at.x_peer)
+
+    def emb_in(s):
+        ref = emb_ref.at[part(s), peer_half]
+        return send(ref, ref, e_s.at[s], e_r.at[s], at.x_peer)
+
     load(ox).wait()
-    ev[0] = embed(ox)
+    embed(ox)
     load(x).start()
-    emb_send = send(ev.at[0], emb_ref.at[:, own_cols], e_sem.at[0], e_sem.at[1], at.x_peer)
 
     def to_x(s):
         return send(dv.at[c, ox, s], xb.at[s], c_s.at[s], c_r.at[s], at.x_peer)
@@ -392,6 +574,7 @@
             dv[c, :, s].astype(F32) + ra[y, :, s].astype(F32) + yb[:, s].astype(F32)
         ).astype(BF16)
         to_x(s).start()
+        emb_piece(s).start()
 
     def back(s):
         return send(rb.at[s], t_ref.at[e], t_s.at[s], t_r.at[e], (s, k, y))
@@ -408,45 +591,53 @@
         def _():
             back(s).start()
 
+    fold_y(0)
     load(x).wait()
-    ev[1] = embed(x)
-    keep = pltpu.make_async_copy(ev.at[1], emb_ref.at[:, own_cols], l_sem.at[0])
+    embed(x)
+    keep = pltpu.make_async_copy(ev.at[x], emb_ref.at[:, own_half], l_sem.at[0])
     keep.start()
-
-    fold_y(0)
-    emb_send.start()
 
     def step(s):
         fold_y(s)
         fold_x(s - 1)
 
-    lax.fori_loop(1, senders, lambda i, carry: (step(i), carry)[1], 0)
+    lax.fori_loop(1, senders // 2 - 1, lambda i, carry: (step(i), carry)[1], 0)
+    for i in range(1, chips - 1):
+        relay(i, True)
+    for i in range(chips - 1):
+        relay(i, False)
+    lax.fori_loop(senders // 2 - 1, senders, lambda i, carry: (step(i), carry)[1], 0)
     fold_x(senders - 1)
-
-    def came(i):
+    settle()
+
+    def returned(i):
         s = at.other(i)
         send(rb.at[s], t_ref.at[s], t_s.at[s], t_r.at[s], (s, k, y)).wait_recv()
         back(s).wait_send()
 
-    lax.fori_loop(1, senders, lambda i, carry: (came(i), carry)[1], 0)
+    loop(senders, returned, 1)
 
     def sent(s):
         core(oy, s).wait_send()
         core(y, s).wait_send()
         across(s).wait_send()
         to_x(s).wait_send()
-
-    over(sent)
-    emb_send.wait_send()
-    send(
-        ev.at[0], emb_ref.at[:, pl.ds(pl.multiple_of(ox * half, LANES), half)], e_sem.at[0], e_sem.at[1], at.x_peer
-    ).wait_recv()
+        emb_piece(s).wait_send()
+        emb_in(s).wait_recv()
+
+    loop(senders, sent)
+    line.visit(groups - 2, line.room, lambda way, b: w_hop(way, b).wait_send())
     keep.wait()
-
-
-def finish(shared, weight, grads):
+    sums_sent()
+    swap.wait_send()
+    swap_in.wait_recv()
+    swap_keep.wait()
+
+
+def finish(shared, weight, grads, partial):
     groups, _, senders, most, width = shared.shape
     _, rows, half = grads.shape
+    chips = partial.shape[0]
     dma = pltpu.SemaphoreType.DMA
     any_spec = pl.BlockSpec(memory_space=pl.ANY)
     vmem = pl.BlockSpec(memory_space=pltpu.VMEM)
@@ -455,11 +646,16 @@
         out_shape=(
             jax.ShapeDtypeStruct((rows, 2 * half), BF16),
             jax.ShapeDtypeStruct((senders, most, width), BF16),
+            jax.ShapeDtypeStruct((weight.shape[1], 2 * half), BF16),
         ),
-        in_specs=[any_spec, vmem, vmem],
-        out_specs=(any_spec, vmem),
+        in_specs=[any_spec, any_spec, vmem, any_spec],
+        out_specs=(any_spec, vmem, any_spec),
         scratch_shapes=[
+            pltpu.VMEM((chips + 1, *partial.shape[1:]), BF16),
+            pltpu.VMEM((2, *partial.shape[1:]), BF16),
+            dma((2, 2)), dma((2, chips, 2)), dma((2, chips, 2)), dma((2,)), dma((1,)),
             pltpu.VMEM((groups, senders, most, width), BF16),
+            pltpu.VMEM(weight.shape, BF16),
             pltpu.VMEM((groups, 2, senders, most, width), BF16),
             pltpu.VMEM((2, 2, senders, most, width), BF16),
             pltpu.VMEM((2, senders, most, width), BF16),
@@ -468,16 +664,17 @@
             pltpu.VMEM((2, rows, half), BF16),
             dma((2, senders)), dma((2, senders)), dma((senders,)), dma((senders,)),
             dma((senders,)), dma((senders,)), dma((senders,)), dma((senders,)),
-            dma((2,)), dma((1,)), dma((1,)),
+            dma((senders,)), dma((senders,)), dma((1,)), dma((1,)),
+            dma((2, senders)), dma((senders,)), dma((groups,)),
         ],
         compiler_params=pltpu.CompilerParams(
-            collective_id=1, has_side_effects=True, vmem_limit_bytes=62 * 1024 * 1024
+            collective_id=1, has_side_effects=True, vmem_limit_bytes=67043328
         ),
         cost_estimate=pl.CostEstimate(
             flops=60 * 10**9, bytes_accessed=32 * rows * half, transcendentals=0
         ),
         name="finish",
-    )(shared, weight, grads)
+    )(shared, weight, grads, partial)
 
 
 def row_kernel(mine, total, seen, send_sem, recv_sem):
@@ -602,13 +799,6 @@
     width = gain.shape[0]
     senders = lax.axis_size("enc")
     most_slots = embed_grad.shape[0] // senders
-    block = 2
-    near = [[b * block + i for i in range(block)] for b in range(senders // block)]
-    far = [[b * block + i for b in range(senders // block)] for i in range(block)]
-
-    def near_exchange(v, split, concat):
-        return lax.all_to_all(v, "enc", split, concat, axis_index_groups=near, tiled=True)
-
     groups = width // owned_width
     column_start = lax.axis_index(features) * owned_width
     gain_own = lax.dynamic_slice_in_dim(gain, column_start, owned_width, 0)
@@ -628,14 +818,11 @@
     grad_partial, shared, grads, weight = spread(
         outgoing.reshape(senders, most_slots, owned_width), embed_grad, proj_weight
     )
-    grad_part = lax.psum_scatter(
-        grad_partial, "enc", scatter_dimension=0, axis_index_groups=far, tiled=True
-    )
-    grad_weight = near_exchange(grad_part, 0, 1).astype(F32)
-
-    embeds_recv, returned = finish(
-        shared, weight.reshape(groups, owned_width, weight.shape[2]), grads
-    )
+    embeds_recv, returned, grad_sum = finish(
+        shared, weight, grads,
+        grad_partial.reshape(senders // 2, 2, weight.shape[1], weight.shape[2]),
+    )
+    grad_weight = grad_sum.astype(F32)
     dnormed = lax.dot_general(
         chosen, returned.reshape(senders * most_slots, owned_width), (((0,), (0,)), ((), ())),
         preferred_element_type=F32,

time: 360 us -> 317 us (0.88); the launches traced: 359 us -> 312 us
  Pallas kernels: 318 us -> 288 us
  between operations: 14.1 us -> 0.8 us
  starting transfers between devices: 5.24 us -> 0 us
    pallas_call x1, Pallas kernels: 147 us -> 122 us  [spread(): pl.pallas_call(spread_kernel, out_shape=(jax.ShapeDtypeStruct((groups * w...]
    pallas_call x1, Pallas kernels: 21 us -> 10.2 us  [sum_both(): pl.pallas_call(both_kernel, out_shape=(jax.ShapeDtypeStruct(rows.shape, F...]
    pallas_call x1, Pallas kernels: 145 us -> 151 us  [finish(): pl.pallas_call(finish_kernel, out_shape=(jax.ShapeDtypeStruct((rows, 2 *...]
    all_to_all x1 -> x0, starting transfers between devices: 5.2 us -> none  [near_exchange(): lax.all_to_all(v, 'enc', split, concat, axis_index_groups=near, tiled=True)]
  transfers between devices with their start and end apart: 2 -> 0, of which waited for: 0 -> 0; matrix products, arithmetic and copies ran while one was open for 2% -> 0% of each run, Pallas kernels for 46% -> 0%
where the time goes in v3:
time: 317 us; the launch traced here: 312 us
  Pallas kernels  288 us (91%)
  other arithmetic  10.3 us (3%)
  local copies, waits for them, and re-layouts  7.96 us (3%)
  matrix products  4.22 us (1%)
    pallas_call x1, Pallas kernels, finish(): pl.pallas_call(finish_kernel, out_shape=(jax.ShapeDtypeStruct((rows, 2 *...  151 us
    pallas_call x1, Pallas kernels, spread(): pl.pallas_call(spread_kernel, out_shape=(jax.ShapeDtypeStruct((groups * w...  122 us
    pallas_call x1, Pallas kernels, sum_both(): pl.pallas_call(both_kernel, out_shape=(jax.ShapeDtypeStruct(rows.shape, F...  10.2 us

profile of v3, /device:TPU:28, one launch (start us, length us, event | category | flops | bytes accessed | tf_op | source)
XLA Modules:
  0.0 311.7 jit_solution(13957685091933569808)
XLA Ops:
  0.6 1.2 convert_reduce_fusion
  1.8 0.6 pad_maximum_fusion.1.mine
  2.4 4.9 %sum_rows.1 = f32[2,256]{1,0:T(2,128)} custom-call(f32[2,256]{1,0:T(2,128)} %pad_maximum_fusion.1.mine), custom_call_target="tpu_custom_call" | custom-call | tf_op jit(solution)/shard_map/sum_rows/pallas_call | solution.py:713
  7.3 0.8 slice_multiply_fusion.3
  8.1 0.8 dynamic_slice.6
  8.9 0.8 dynamic_slice.7
  9.7 0.7 fusion.23
  10.4 0.6 reduce-window.6
  11.2 0.8 fusion.22
  12.0 0.7 multiply_add_fusion
  13.2 1.6 convolution_convert_fusion
  14.8 1.6 copy.12
  16.4 122.3 %spread.1 = (bf16[3200,1024]{1,0:T(8,128)(2,1)}, bf16[4,2,8,96,800]{4,3,2,1,0:T(8,128)(2,1)}, bf16[2,768,1024]{2,1,0:T(8,128)(2,1)}, bf16[8,400,1024]{2,1,0:T(8,128)(2,1)}) custom-call(bf16[8,96,800]{2,1,0:T(8,128)(2,1)} %bitcast.22, bf16[768,2048]{1,0:T(8,128)(2,1)} %eg_ref.1, bf16[400,2048]{1,0:T(8,128)(2,1)} %w_ref.1), custom_call_target="tpu_custom_call" | custom-call | flops 60000002048 | bytes 25165824 | tf_op jit(solution)/shard_map/spread/pallas_call | solution.py:310
  138.7 151.0 %finish.1 = (bf16[768,2048]{1,0:T(8,128)(2,1)}, bf16[8,96,800]{2,1,0:T(8,128)(2,1)}, bf16[400,2048]{1,0:T(8,128)(2,1)}) custom-call(bf16[4,2,8,96,800]{4,3,2,1,0:T(8,128)(2,1)} %get-tuple-element.14.n_ref, bf16[8,400,1024]{2,1,0:T(8,128)(2,1)} %get-tuple-element.15.wg_ref, bf16[2,768,1024]{2,1,0:T(8,128)(2,1)} %get-tuple-element.16.eg_ref, ...), custom_call_target="tpu_custom_call" | custom-call | flops 60000002048 | bytes 25165824 | tf_op jit(solution)/shard_map/finish/pallas_call | solution.py:644
  289.8 2.6 fusion.9
  292.4 0.6 pad_maximum_fusion.2.mine
  293.0 0.6 pad_maximum_fusion.mine_cols
  293.6 10.2 %sum_both.1 = (f32[2,256]{1,0:T(2,128)}, f32[2,800]{1,0:T(2,128)}) custom-call(f32[2,256]{1,0:T(2,128)} %pad_maximum_fusion.2.mine, f32[2,800]{1,0:T(2,128)} %pad_maximum_fusion.mine_cols), custom_call_target="tpu_custom_call" | custom-call | tf_op jit(solution)/shard_map/sum_both/pallas_call | solution.py:778
  303.8 0.7 slice_multiply_fusion.1
  304.5 1.0 fusion.12
  305.5 1.4 slice_reduce_fusion.1
  306.9 2.1 convert_element_type.29
  309.0 1.0 copy-done
  310.0 1.7 copy.14
  (25 shorter events, 0.9 us)
Async XLA Ops:
  8.1 130.6 %copy-start.5 = (f32[1,256]{1,0:T(1,128)}, f32[1,256]{1,0:T(1,128)S(1)}, u32[]{:S(2)}) copy-start(f32[1,256]{1,0:T(1,128)S(1)} %get-tuple-element.33) | copy-start | bytes 3076
  8.1 130.6 %copy-start.7 = (f32[256]{0:T(256)}, f32[256]{0:T(256)S(1)}, u32[]{:S(2)}) copy-start(f32[256]{0:T(256)S(1)} %add_rsqrt_fusion) | copy-start | bytes 3076
  8.9 129.8 %copy-start.3 = (f32[800]{0:T(1024)}, f32[800]{0:T(1024)S(1)}, u32[]{:S(2)}) copy-start(f32[800]{0:T(1024)S(1)} %dynamic_slice.6) | copy-start | bytes 9604
  12.6 0.6 copy-start.9
  289.8 14.8 %copy-start.2 = (bf16[256,800]{0,1:T(8,128)(2,1)S(1)}, bf16[256,800]{0,1:T(8,128)(2,1)}, u32[]{:S(2)}) copy-start(bf16[256,800]{0,1:T(8,128)(2,1)} %param.6) | copy-start | bytes 1228804
  289.8 14.8 %copy-start.4 = (f32[800]{0:T(1024)S(1)}, f32[800]{0:T(1024)}, u32[]{:S(2)}) copy-start(f32[800]{0:T(1024)} %copy-done.3) | copy-start | bytes 9604
  289.8 14.7 %copy-start.6 = (f32[1,256]{1,0:T(1,128)S(1)}, f32[1,256]{1,0:T(1,128)}, u32[]{:S(2)}) copy-start(f32[1,256]{1,0:T(1,128)} %copy-done.5) | copy-start | bytes 3076
  289.8 14.7 %copy-start.8 = (f32[256]{0:T(256)S(1)}, f32[256]{0:T(256)}, u32[]{:S(2)}) copy-start(f32[256]{0:T(256)} %copy-done.7) | copy-start | bytes 3076
  289.8 17.1 %copy-start.1 = (bf16[400,2048]{1,0:T(8,128)(2,1)S(1)}, bf16[400,2048]{1,0:T(8,128)(2,1)}, u32[]{:S(2)}) copy-start(bf16[400,2048]{1,0:T(8,128)(2,1)} %get-tuple-element.21) | copy-start | bytes 4915204
  306.9 3.1 copy-start

commit v4 on v3

--- a/solution.py
+++ b/solution.py
@@ -92,8 +92,8 @@
     def block(self, way, distance, parity):
         return 2 * (self.z - distance if way == 0 else self.z + distance) + parity
 
-    def visit(self, distance, condition, fn):
-        for parity in self.parities:
+    def visit(self, distance, condition, fn, parities=None):
+        for parity in self.parities if parities is None else parities:
             for way in range(2):
                 @pl.when(condition(way, distance))
                 def _():
@@ -102,7 +102,7 @@
 
 def spread_kernel(
     out_ref, eg_ref, w_ref, gw_ref, n_ref, eg_out, wg_ref,
-    nv, eg_v, wl, route_s, route_r, x_s, x_r, y_s, y_r, d_s, d_r, eg_s, eg_r, local_sem, n_sem, w_x, w_s, w_r,
+    nv, eg_v, wl, acc, route_s, route_r, x_s, x_r, y_s, y_r, d_s, d_r, eg_s, eg_r, local_sem, n_sem, w_x, w_s, w_r,
 ):
     at = Place()
     line = Line(at)
@@ -177,7 +177,7 @@
             def _():
                 w_hop(way, b, src).start()
 
-    def w_relay(distance, last):
+    def w_relay(distance, last, parities=None):
         def one(way, b):
             w_hop(way, b).wait_recv()
             if not last:
@@ -185,7 +185,7 @@
                 def _():
                     w_hop(way, b).start()
 
-        line.visit(distance, line.came, one)
+        line.visit(distance, line.came, one, parities)
 
     eg_load.start()
     w_load.start()
@@ -204,7 +204,6 @@
 
     for w in range(2):
         pass_on(z, w, out_ref.at[2 * z + w])
-        eg_piece(w).start()
         nv[c, w, e] = out_ref[2 * z + w]
 
     def pass_route(i):
@@ -212,11 +211,12 @@
         for w in range(2):
             route_in(s, w).wait_recv()
             pass_on(s, w, nv.at[c, w, 2 * s + x])
-            eg_piece(2 * i + w).start()
 
     loop(chips, pass_route, 1)
+    loop(senders, lambda i: eg_piece(i).start())
     w_swap_in.wait_recv()
     w_own(e_peer, wg_ref.at[e_peer])
+    w_relay(1, groups == 3, (x,))
 
     def pass_x(i):
         s = chip(i)
@@ -227,7 +227,7 @@
             k_hop(y, 2 * s + ox, w, ref).start()
 
     loop(chips, pass_x)
-    w_relay(1, groups == 3)
+    w_relay(1, groups == 3, (ox,))
 
     def pass_y(parity):
         def one(i):
@@ -245,34 +245,42 @@
 
         loop(senders, one)
 
-    def product(group):
-        total = None
-        for w in range(2):
-            term = lax.dot_general(
-                nv[group, w].reshape(rows, width), eg_v[w], (((0,), (0,)), ((), ())), preferred_element_type=F32
-            )
-            total = term if total is None else total + term
-        gw_ref[pl.ds(pl.multiple_of(group * width, SUBLANES), width), :] = total.astype(BF16)
+    def term(group, w):
+        return lax.dot_general(
+            nv[group, w].reshape(rows, width), eg_v[w], (((0,), (0,)), ((), ())), preferred_element_type=F32
+        )
+
+    def own_term(i, group):
+        acc[i] = term(group, x)
+
+    def peer_term(i, group):
+        gw_ref[pl.ds(pl.multiple_of(group * width, SUBLANES), width), :] = (
+            acc[i] + term(group, ox)
+        ).astype(BF16)
 
     def keep(i, group):
         pltpu.make_async_copy(nv.at[group], n_ref.at[group], n_sem.at[i]).start()
 
+    eg_load.wait()
     pass_y(x)
-    eg_load.wait()
+    keep(0, c)
+    own_term(0, c)
+    wait_core(y)
+    keep(1, c_k)
+    own_term(1, c_k)
+    pass_y(ox)
+    keep(2, c_y)
+    own_term(2, c_y)
     loop(senders, lambda i: eg_in(i).wait_recv())
     eg_keep = pltpu.make_async_copy(eg_v, eg_out, local_sem.at[0])
     eg_keep.start()
-    keep(0, c)
-    product(c)
-    wait_core(y)
-    keep(1, c_k)
-    product(c_k)
-    pass_y(ox)
-    keep(2, c_y)
-    product(c_y)
+    peer_term(0, c)
+    peer_term(1, c_k)
     wait_core(1 - y)
     keep(3, c_ky)
-    product(c_ky)
+    own_term(3, c_ky)
+    peer_term(2, c_y)
+    peer_term(3, c_ky)
     for distance in range(2, groups - 1):
         w_relay(distance, distance == groups - 2)
 
@@ -321,6 +329,7 @@
             pltpu.VMEM((groups, 2, senders, most, width), BF16),
             pltpu.VMEM((2, rows, half), BF16),
             pltpu.VMEM((proj_weight.shape[0], half), BF16),
+            pltpu.VMEM((groups, width, half), F32),
             dma((chips, 2)), dma((chips, 2)), dma((chips, 2)), dma((chips, 2)),
             dma((senders, 2)), dma((senders, 2)), dma((2, senders, 2)), dma((2, senders, 2)),
             dma((senders,)), dma((senders,)), dma((3,)), dma((groups,)), dma((2,)), dma((2, senders)), dma((senders,)),

time: 317 us -> 304 us (0.959)
  Pallas kernels: 288 us -> 276 us
    pallas_call x1, Pallas kernels: 122 us -> 102 us  [spread(): pl.pallas_call(spread_kernel, out_shape=(jax.ShapeDtypeStruct((groups * w...]
    pallas_call x1, Pallas kernels: 151 us -> 159 us  [finish(): pl.pallas_call(finish_kernel, out_shape=(jax.ShapeDtypeStruct((rows, 2 *...]
where the time goes in v4:
time: 304 us; the launch traced here: 299 us
  Pallas kernels  276 us (91%)
  other arithmetic  10.3 us (3%)
  local copies, waits for them, and re-layouts  7.96 us (3%)
  matrix products  4.22 us (1%)
    pallas_call x1, Pallas kernels, finish(): pl.pallas_call(finish_kernel, out_shape=(jax.ShapeDtypeStruct((rows, 2 *...  159 us
    pallas_call x1, Pallas kernels, spread(): pl.pallas_call(spread_kernel, out_shape=(jax.ShapeDtypeStruct((groups * w...  102 us
    pallas_call x1, Pallas kernels, sum_both(): pl.pallas_call(both_kernel, out_shape=(jax.ShapeDtypeStruct(rows.shape, F...  9.75 us

profile of v4, /device:TPU:28, one launch (start us, length us, event | category | flops | bytes accessed | tf_op | source)
XLA Modules:
  0.0 298.8 jit_solution(2631772064155028244)
XLA Ops:
  0.6 1.2 convert_reduce_fusion
  1.8 0.6 pad_maximum_fusion.1.mine
  2.4 4.9 %sum_rows.1 = f32[2,256]{1,0:T(2,128)} custom-call(f32[2,256]{1,0:T(2,128)} %pad_maximum_fusion.1.mine), custom_call_target="tpu_custom_call" | custom-call | tf_op jit(solution)/shard_map/sum_rows/pallas_call | solution.py:722
  7.3 0.8 slice_multiply_fusion.3
  8.1 0.8 dynamic_slice.6
  8.9 0.8 dynamic_slice.7
  9.7 0.7 fusion.23
  10.4 0.6 reduce-window.6
  11.2 0.8 fusion.22
  12.0 0.7 multiply_add_fusion
  13.2 1.6 convolution_convert_fusion
  14.8 1.6 copy.12
  16.4 101.9 %spread.1 = (bf16[3200,1024]{1,0:T(8,128)(2,1)}, bf16[4,2,8,96,800]{4,3,2,1,0:T(8,128)(2,1)}, bf16[2,768,1024]{2,1,0:T(8,128)(2,1)}, bf16[8,400,1024]{2,1,0:T(8,128)(2,1)}) custom-call(bf16[8,96,800]{2,1,0:T(8,128)(2,1)} %bitcast.22, bf16[768,2048]{1,0:T(8,128)(2,1)} %eg_ref.1, bf16[400,2048]{1,0:T(8,128)(2,1)} %w_ref.1), custom_call_target="tpu_custom_call" | custom-call | flops 60000002048 | bytes 25165824 | tf_op jit(solution)/shard_map/spread/pallas_call | solution.py:318
  118.3 158.9 %finish.1 = (bf16[768,2048]{1,0:T(8,128)(2,1)}, bf16[8,96,800]{2,1,0:T(8,128)(2,1)}, bf16[400,2048]{1,0:T(8,128)(2,1)}) custom-call(bf16[4,2,8,96,800]{4,3,2,1,0:T(8,128)(2,1)} %get-tuple-element.14.n_ref, bf16[8,400,1024]{2,1,0:T(8,128)(2,1)} %get-tuple-element.15.wg_ref, bf16[2,768,1024]{2,1,0:T(8,128)(2,1)} %get-tuple-element.16.eg_ref, ...), custom_call_target="tpu_custom_call" | custom-call | flops 60000002048 | bytes 25165824 | tf_op jit(solution)/shard_map/finish/pallas_call | solution.py:653
  277.3 2.6 fusion.9
  279.9 0.6 pad_maximum_fusion.2.mine
  280.5 0.6 pad_maximum_fusion.mine_cols
  281.1 9.7 %sum_both.1 = (f32[2,256]{1,0:T(2,128)}, f32[2,800]{1,0:T(2,128)}) custom-call(f32[2,256]{1,0:T(2,128)} %pad_maximum_fusion.2.mine, f32[2,800]{1,0:T(2,128)} %pad_maximum_fusion.mine_cols), custom_call_target="tpu_custom_call" | custom-call | tf_op jit(solution)/shard_map/sum_both/pallas_call | solution.py:787
  290.9 0.7 slice_multiply_fusion.1
  291.6 1.0 fusion.12
  292.6 1.4 slice_reduce_fusion.1
  294.0 2.1 convert_element_type.29
  296.1 1.0 copy-done
  297.1 1.7 copy.14
  (25 shorter events, 0.9 us)
Async XLA Ops:
  8.1 110.2 %copy-start.5 = (f32[1,256]{1,0:T(1,128)}, f32[1,256]{1,0:T(1,128)S(1)}, u32[]{:S(2)}) copy-start(f32[1,256]{1,0:T(1,128)S(1)} %get-tuple-element.33) | copy-start | bytes 3076
  8.1 110.2 %copy-start.7 = (f32[256]{0:T(256)}, f32[256]{0:T(256)S(1)}, u32[]{:S(2)}) copy-start(f32[256]{0:T(256)S(1)} %add_rsqrt_fusion) | copy-start | bytes 3076
  8.9 109.4 %copy-start.3 = (f32[800]{0:T(1024)}, f32[800]{0:T(1024)S(1)}, u32[]{:S(2)}) copy-start(f32[800]{0:T(1024)S(1)} %dynamic_slice.6) | copy-start | bytes 9604
  12.6 0.6 copy-start.9
  277.3 14.3 %copy-start.2 = (bf16[256,800]{0,1:T(8,128)(2,1)S(1)}, bf16[256,800]{0,1:T(8,128)(2,1)}, u32[]{:S(2)}) copy-start(bf16[256,800]{0,1:T(8,128)(2,1)} %param.6) | copy-start | bytes 1228804
  277.3 14.3 %copy-start.4 = (f32[800]{0:T(1024)S(1)}, f32[800]{0:T(1024)}, u32[]{:S(2)}) copy-start(f32[800]{0:T(1024)} %copy-done.3) | copy-start | bytes 9604
  277.3 14.3 %copy-start.6 = (f32[1,256]{1,0:T(1,128)S(1)}, f32[1,256]{1,0:T(1,128)}, u32[]{:S(2)}) copy-start(f32[1,256]{1,0:T(1,128)} %copy-done.5) | copy-start | bytes 3076
  277.3 14.3 %copy-start.8 = (f32[256]{0:T(256)S(1)}, f32[256]{0:T(256)}, u32[]{:S(2)}) copy-start(f32[256]{0:T(256)} %copy-done.7) | copy-start | bytes 3076
  277.3 16.7 %copy-start.1 = (bf16[400,2048]{1,0:T(8,128)(2,1)S(1)}, bf16[400,2048]{1,0:T(8,128)(2,1)}, u32[]{:S(2)}) copy-start(bf16[400,2048]{1,0:T(8,128)(2,1)} %get-tuple-element.21) | copy-start | bytes 4915204
  294.0 3.1 %copy-start = (bf16[768,2048]{1,0:T(8,128)(2,1)S(1)}, bf16[768,2048]{1,0:T(8,128)(2,1)}, u32[]{:S(2)}) copy-start(bf16[768,2048]{1,0:T(8,128)(2,1)} %get-tuple-element.41) | copy-start | bytes 9437188
